TPU v7x, 128 devices: a whole 4x4x4 slice. The times are simulated.
128 devices in a mesh: rows: 128 (over y, x, z, core).
Axes of the slice: x: 4, y: 4, z: 4, core: 2. Of those that a mesh axis runs over, the one named last changes fastest.
Arguments:
- blocks: float32 [2048, 4, 256, 256], P('rows'), may hold values from -0.125 to 0.125
- block_cols: int32 [2048, 4], P('rows'), may hold values from 0 to 2047, as said below
- live_counts: int32 [2048], P('rows'), may hold values from 1 to 4, as said below
- onsite_energy: float32 [524288], P('rows'), may hold values from -2 to 2
- precond: float32 [2048, 256, 256], P('rows')
- vectors: float32 [32, 524288], P(None, 'rows'), may hold values from -6 to 6
- prev_vectors: float32 [32, 524288], P(None, 'rows'), may hold values from -6 to 6
- prev_image: float32 [32, 524288], P(None, 'rows'), may hold values from -6 to 6
Outputs:
- correction: float32 [32, 524288], P(None, 'rows')
- reduced: float32 [96, 96], replicated
Inputs may be any that keep to these rules, and one draw needn't show every extreme that they name: block_cols[b, s] = (b + o) mod 2048, with the offsets o of one block-row distinct and within 0 to 4; every slot holds a valid block-column. Slots s < live_counts[b] are live, the rest are ignored; some block-row has 4 live slots in every draw.
All inputs are finite; a program needn't handle non-finite values.
Results may differ from a plain program's by a relative error of at most 0.00026.
Values sent between devices are 32-bit elements; how exact they have to be, the bound alone decides.
A program may use at most 128 MiB of HBM per device.

v0:
```python
import jax
import jax.numpy as jnp
from jax import lax
from jax.sharding import Mesh
from jax.sharding import PartitionSpec as P

HB = 4
ITERS = 3
ROWS = ("rows_0", "rows_1", "rows_2", "rows_3")


def shifted(block, axis, distance):
    devices = range(lax.axis_size(axis))
    route = [((i - distance) % len(devices), i) for i in devices]
    return lax.ppermute(block, axis, route)


def copy_for_each(shard, axis):
    count = lax.axis_size(axis)
    return lax.all_to_all(
        jnp.broadcast_to(shard[None], (count, *shard.shape)), axis, 0, 0, tiled=True
    )


def of_everyone(shard, axis):
    everything = copy_for_each(shard, axis)
    return jnp.sum(everything, axis=0)


def by_axis(shard, axes):
    far, near = axes
    nearer = of_everyone(shard, near)
    return of_everyone(nearer, far)


def in_one(arrays, axis):
    line, at, done = (jnp.concatenate([a.reshape(-1) for a in arrays]), 0, [])
    running = by_axis(line, axis)
    for a in arrays:
        done.append(running[at : at + a.size].reshape(a.shape))
        at += a.size
    return tuple(done)


def padded_apply(source, tiles, offsets, counts_here, extended, extent):
    slot_count = tiles.shape[1]
    live_mask = (
        lax.broadcasted_iota(jnp.int32, (tiles.shape[0], slot_count), 1) < counts_here[:, None]
    ).astype(jnp.float32)
    one_hot = (offsets[:, :, None] == lax.broadcasted_iota(jnp.int32, (1, 1, extent), 2)).astype(
        jnp.float32
    ) * live_mask[:, :, None]
    moved = jnp.einsum("kbi,bsij->kbsj", source, tiles, precision=lax.Precision.HIGHEST)
    spread = jnp.einsum("bse,kbsj->kej", one_hot, moved, precision=lax.Precision.HIGHEST)
    forward_part = None
    picked = jnp.einsum("bse,kej->kbsj", one_hot, extended, precision=lax.Precision.HIGHEST)
    forward_part = jnp.einsum("bsij,kbsj->kbi", tiles, picked, precision=lax.Precision.HIGHEST)
    return (forward_part, spread)


def apply_tiles(source, tiles, offsets, counts_here, extended, extent):
    return padded_apply(source, tiles, offsets, counts_here, extended, extent)


def local(
    blocks, block_cols, live_counts, onsite_energy, precond, vectors, prev_vectors, prev_image
):
    block_rows = blocks.shape[0]
    block_size = blocks.shape[2]
    vec_count = vectors.shape[0]
    local_rows = block_rows * block_size
    reach = HB
    total_blocks = block_rows * lax.axis_size(ROWS)
    first_block = lax.axis_index(ROWS) * block_rows
    own_offsets = (block_cols - first_block) % total_blocks

    def operate(field):
        source = field.reshape(vec_count, block_rows, block_size)
        right_rows = shifted(field[:, : reach * block_size], ROWS, -1)
        extended = jnp.concatenate([field, right_rows], axis=1).reshape(
            vec_count, block_rows + reach, block_size
        )
        forward_part, spread = apply_tiles(
            source, blocks, own_offsets, live_counts, extended, block_rows + reach
        )
        outgoing = spread[:, block_rows:].reshape(vec_count, reach * block_size)
        incoming = shifted(outgoing, ROWS, 1)
        own_part = spread[:, :block_rows].reshape(vec_count, local_rows)
        own_part = own_part + jnp.pad(incoming, ((0, 0), (0, local_rows - reach * block_size)))
        return (
            onsite_energy[None, :] * field + forward_part.reshape(vec_count, local_rows) + own_part
        )

    image = operate(vectors)
    leading = jnp.concatenate([vectors, prev_vectors], axis=0)
    numerator_part = jnp.sum(vectors * image, axis=1)
    denominator_part = jnp.sum(vectors * vectors, axis=1)
    lead_image = jnp.concatenate([image, prev_image], axis=0)
    numerator, denominator, gram_lead, proj_lead = in_one(
        (
            numerator_part,
            denominator_part,
            jnp.dot(leading, leading.T, precision=lax.Precision.HIGHEST),
            jnp.dot(leading, lead_image.T, precision=lax.Precision.HIGHEST),
        ),
        (("rows_0", "rows_1"), ("rows_2", "rows_3")),
    )
    quotient = numerator / denominator
    remainder = -(image - quotient[:, None] * vectors)
    correction = jnp.zeros_like(vectors)
    hcorr = jnp.zeros_like(vectors)
    for iteration in range(ITERS):
        shaped = remainder.reshape(vec_count, block_rows, block_size)
        search = jnp.einsum(
            "bij,kbj->kbi", precond, shaped, precision=lax.Precision.HIGHEST
        ).reshape(vec_count, local_rows)
        applied = operate(search) - quotient[:, None] * search
        cross_sum, self_sum = in_one(
            (jnp.sum(applied * remainder, axis=1), jnp.sum(applied * applied, axis=1)),
            (("rows_0", "rows_1", "rows_2"), "rows_3"),
        )
        step_size = cross_sum / (self_sum + 1.0)
        correction = correction + step_size[:, None] * search
        hcorr = hcorr + step_size[:, None] * (applied + quotient[:, None] * search)
        remainder = remainder - step_size[:, None] * applied
    basis = jnp.concatenate([vectors, prev_vectors, correction], axis=0)
    himage = jnp.concatenate([image, prev_image, hcorr], axis=0)
    gram_tail, proj_tail, proj_side = in_one(
        (
            jnp.dot(correction, basis.T, precision=lax.Precision.HIGHEST),
            jnp.dot(correction, himage.T, precision=lax.Precision.HIGHEST),
            jnp.dot(leading, hcorr.T, precision=lax.Precision.HIGHEST),
        ),
        (("rows_0", "rows_1"), ("rows_2", "rows_3")),
    )
    lead_count = leading.shape[0]
    gram_top = jnp.concatenate([gram_lead, gram_tail[:, :lead_count].T], axis=1)
    gram_matrix = jnp.concatenate([gram_top, gram_tail], axis=0)
    proj_top = jnp.concatenate([proj_lead, proj_side], axis=1)
    projected = jnp.concatenate([proj_top, proj_tail], axis=0)
    gram_matrix = gram_matrix + jnp.eye(gram_matrix.shape[0], dtype=jnp.float32)
    factor = jnp.linalg.cholesky(gram_matrix)
    half_way = jax.scipy.linalg.solve_triangular(factor, projected, lower=True)
    reduced = jax.scipy.linalg.solve_triangular(factor, half_way.T, lower=True).T
    return (correction, reduced)


def solution(mesh):
    torus = Mesh(mesh.devices.reshape(4, 4, 4, 2), ("rows_0", "rows_1", "rows_2", "rows_3"))
    return jax.shard_map(
        local,
        mesh=torus,
        in_specs=(
            P(ROWS, None, None, None),
            P(ROWS, None),
            P(ROWS),
            P(ROWS),
            P(ROWS, None, None),
            P(None, ROWS),
            P(None, ROWS),
            P(None, ROWS),
        ),
        out_specs=(P(None, ROWS), P()),
        check_vma=False,
    )
```

profile of v0, /device:TPU:0, one launch (start us, length us, event | category | flops | bytes accessed | tf_op | source)
XLA Modules:
  0.0 360.0 jit_solution(14653472068718500510)
XLA Ops:
  0.6 0.9 slice.114
  1.5 8.3 %collective-permute-start = (f32[32,1024]{1,0:T(8,128)S(1)}, f32[32,1024]{1,0:T(8,128)S(1)}, u32[]{:S(2)}, u32[]{:S(2)}) collective-permute-start(f32[32,1024]{1,0:T(8,128)S(1)} %slice.114), channel_id=1, source_target_pairs={{1,0},{2,1},{3,2},{4,3},{5,4},{6,5},{7,6},{8,7},{9,8},{10,9},{11,1... | collective-permute-start | bytes 393224 | tf_op jit(solution)/shard_map/ppermute | solution.py:15
  10.5 1.2 copy.126
  11.7 0.7 add_select_fusion
  12.4 13.9 %convolution_bitcast_fusion.6 = f32[32,16,4,256]{3,0,2,1:T(8,128)S(1)} fusion(f32[16,4,256,256]{3,2,1,0:T(8,128)} %param.10, f32[32,16,256,1]{2,1,0,3:T(8,128)S(1)} %bitcast.216), kind=kOutput, calls=%fused_computation.22 | convolution fusion | flops 1610612736 | bytes 19398656 | tf_op jit(solution)/shard_map/kbi,bsij->kbsj/dot_general | solution.py:53
  26.3 2.4 fusion.28
  29.7 1.8 convolution_bitcast_fusion.7
  31.5 18.8 %fusion.40 = f32[16,4,8,256]{3,2,1,0:T(8,128)S(1)} fusion(f32[16,4,256,256]{3,2,1,0:T(8,128)} %param.10, f32[32,16,4,256]{3,1,2,0:T(8,128)S(1)} %convolution_bitcast_fusion.7), kind=kOutput, calls=%fused_computation.40 | convolution fusion | flops 1610612736 | bytes 19398656 | tf_op jit(solution)/shard_map/bsij,kbsj->kbi/dot_general | solution.py:57
  51.4 1.0 fusion.138
  52.3 1.0 fusion.52
  53.7 10.0 %all_to_all.60 = f32[8,1,8256]{2,1,0:T(1,128)S(1)} all-to-all(f32[8,1,8256]{2,1,0:T(1,128)S(1)} %broadcast_in_dim.21), channel_id=1, replica_groups=mesh['rows_0'=4,'rows_1'=4,'rows_2'=4,'rows_3'=2] {'rows_2','rows_3'}, dimensions={0} | all-to-all | bytes 528384 | tf_op jit(solution)/shard_map/all_to_all | solution.py:20
  64.3 20.0 %all_to_all.61 = f32[16,1,8256]{2,1,0:T(1,128)S(1)} all-to-all(f32[16,1,8256]{2,1,0:T(1,128)S(1)} %broadcast_in_dim.22), channel_id=1, replica_groups=mesh['rows_0'=4,'rows_1'=4,'rows_2'=4,'rows_3'=2] {'rows_0','rows_1'}, dimensions={0} | all-to-all | bytes 1056768 | tf_op jit(solution)/shard_map/all_to_all | solution.py:20
  84.8 6.1 %fusion.66 = f32[16,32,256]{2,1,0:T(8,128)S(1)} fusion(f32[16,256,256]{2,1,0:T(8,128)} %param.14, f32[4,16,8,256]{3,2,1,0:T(8,128)S(1)} %bitcast.210), kind=kOutput, calls=%fused_computation.64 | convolution fusion | flops 402653184 | bytes 5242880 | tf_op jit(solution)/shard_map/bij,kbj->kbi/dot_general | solution.py:114
  90.9 13.0 %convolution_bitcast_fusion.4 = f32[32,16,4,256]{3,0,2,1:T(8,128)S(1)} fusion(f32[16,4,256,256]{3,2,1,0:T(8,128)} %param.10, f32[16,32,256]{2,1,0:T(8,128)S(1)} %fusion.66), kind=kOutput, calls=%fused_computation.20 | convolution fusion | flops 1610612736 | bytes 19398656 | tf_op jit(solution)/shard_map/kbi,bsij->kbsj/dot_general | solution.py:53
  103.9 0.8 collective-permute-start.2
  104.8 2.4 fusion.31
  107.3 1.1 copy.129
  109.3 0.9 pad_maximum_fusion.1
  110.1 1.2 reshape.257
  111.3 1.8 convolution_bitcast_fusion.5
  113.2 18.8 %fusion.43 = f32[16,4,8,256]{3,2,1,0:T(8,128)S(1)} fusion(f32[16,4,256,256]{3,2,1,0:T(8,128)} %param.10, f32[32,16,4,256]{3,1,2,0:T(8,128)S(1)} %convolution_bitcast_fusion.5), kind=kOutput, calls=%fused_computation.41 | convolution fusion | flops 1610612736 | bytes 19398656 | tf_op jit(solution)/shard_map/bsij,kbsj->kbi/dot_general | solution.py:57
  132.1 2.0 multiply_reduce_fusion.5
  134.2 3.7 %all_to_all.62 = f32[2,1,64]{2,1,0:T(1,128)S(1)} all-to-all(f32[2,1,64]{2,1,0:T(1,128)S(1)} %broadcast_in_dim.23), channel_id=1, replica_groups=mesh['rows_0'=4,'rows_1'=4,'rows_2'=4,'rows_3'=2] {'rows_3'}, dimensions={0} | all-to-all | bytes 1024 | tf_op jit(solution)/shard_map/all_to_all | solution.py:20
  137.9 19.0 %all_to_all.63 = f32[64,1,64]{2,1,0:T(1,128)S(1)} all-to-all(f32[64,1,64]{2,1,0:T(1,128)S(1)} %broadcast_in_dim.24), channel_id=1, replica_groups=mesh['rows_0'=4,'rows_1'=4,'rows_2'=4,'rows_3'=2] {'rows_0','rows_1','ro..., dimensions={0} | all-to-all | bytes 32768 | tf_op jit(solution)/shard_map/all_to_all | solution.py:20
  157.0 1.2 multiply_subtract_fusion.1
  158.2 6.1 %fusion.63 = f32[16,32,256]{2,1,0:T(8,128)S(1)} fusion(f32[16,256,256]{2,1,0:T(8,128)} %param.14, f32[4,16,8,256]{3,2,1,0:T(8,128)S(1)} %bitcast.209), kind=kOutput, calls=%fused_computation.61 | convolution fusion | flops 402653184 | bytes 5242880 | tf_op jit(solution)/shard_map/bij,kbj->kbi/dot_general | solution.py:114
  164.3 13.0 %convolution_bitcast_fusion.2 = f32[32,16,4,256]{3,0,2,1:T(8,128)S(1)} fusion(f32[16,4,256,256]{3,2,1,0:T(8,128)} %param.10, f32[16,32,256]{2,1,0:T(8,128)S(1)} %fusion.63), kind=kOutput, calls=%fused_computation.18 | convolution fusion | flops 1610612736 | bytes 19398656 | tf_op jit(solution)/shard_map/kbi,bsij->kbsj/dot_general | solution.py:53
  177.3 0.8 collective-permute-start.4
  178.1 2.4 fusion.34
  180.6 1.1 copy.131
  181.7 0.7 copy.132
  182.8 0.9 pad_maximum_fusion.2
  183.7 2.1 reshape.261
  185.8 3.0 convolution_bitcast_fusion.3
  188.8 18.8 %fusion.46 = f32[16,4,8,256]{3,2,1,0:T(8,128)S(1)} fusion(f32[16,4,256,256]{3,2,1,0:T(8,128)} %param.10, f32[32,16,4,256]{3,1,2,0:T(8,128)S(1)} %convolution_bitcast_fusion.3), kind=kOutput, calls=%fused_computation.42 | convolution fusion | flops 1610612736 | bytes 19398656 | tf_op jit(solution)/shard_map/bsij,kbsj->kbi/dot_general | solution.py:57
  207.7 1.1 multiply_reduce_fusion.3
  208.8 3.7 %all_to_all.64 = f32[2,1,64]{2,1,0:T(1,128)S(1)} all-to-all(f32[2,1,64]{2,1,0:T(1,128)S(1)} %broadcast_in_dim.25), channel_id=1, replica_groups=mesh['rows_0'=4,'rows_1'=4,'rows_2'=4,'rows_3'=2] {'rows_3'}, dimensions={0} | all-to-all | bytes 1024 | tf_op jit(solution)/shard_map/all_to_all | solution.py:20
  212.6 19.0 %all_to_all.65 = f32[64,1,64]{2,1,0:T(1,128)S(1)} all-to-all(f32[64,1,64]{2,1,0:T(1,128)S(1)} %broadcast_in_dim.26), channel_id=1, replica_groups=mesh['rows_0'=4,'rows_1'=4,'rows_2'=4,'rows_3'=2] {'rows_0','rows_1','ro..., dimensions={0} | all-to-all | bytes 32768 | tf_op jit(solution)/shard_map/all_to_all | solution.py:20
  231.7 1.2 multiply_subtract_fusion
  232.9 0.8 copy-done.3
  233.6 6.1 %fusion.60 = f32[16,32,256]{2,1,0:T(8,128)S(1)} fusion(f32[16,256,256]{2,1,0:T(8,128)} %param.14, f32[4,16,8,256]{3,2,1,0:T(8,128)S(1)} %bitcast.214), kind=kOutput, calls=%fused_computation.58 | convolution fusion | flops 402653184 | bytes 5242880 | tf_op jit(solution)/shard_map/bij,kbj->kbi/dot_general | solution.py:114
  239.7 13.0 %convolution_bitcast_fusion = f32[32,16,4,256]{3,0,2,1:T(8,128)S(1)} fusion(f32[16,4,256,256]{3,2,1,0:T(8,128)} %param.10, f32[16,32,256]{2,1,0:T(8,128)S(1)} %fusion.60), kind=kOutput, calls=%fused_computation.16 | convolution fusion | flops 1610612736 | bytes 19398656 | tf_op jit(solution)/shard_map/kbi,bsij->kbsj/dot_general | solution.py:53
  252.8 0.8 collective-permute-start.6
  253.5 2.4 fusion.37
  256.0 1.1 copy.133
  257.1 0.7 copy.134
  258.0 0.9 pad_maximum_fusion.3
  258.9 2.1 reshape.265
  261.0 3.0 convolution_bitcast_fusion.1
  264.0 18.8 %fusion.49 = f32[16,4,8,256]{3,2,1,0:T(8,128)S(1)} fusion(f32[16,4,256,256]{3,2,1,0:T(8,128)} %param.10, f32[32,16,4,256]{3,1,2,0:T(8,128)S(1)} %convolution_bitcast_fusion.1), kind=kOutput, calls=%fused_computation.43 | convolution fusion | flops 1610612736 | bytes 19398656 | tf_op jit(solution)/shard_map/bsij,kbsj->kbi/dot_general | solution.py:57
  282.9 1.1 multiply_reduce_fusion.1
  284.1 3.7 %all_to_all.66 = f32[2,1,64]{2,1,0:T(1,128)S(1)} all-to-all(f32[2,1,64]{2,1,0:T(1,128)S(1)} %broadcast_in_dim.27), channel_id=1, replica_groups=mesh['rows_0'=4,'rows_1'=4,'rows_2'=4,'rows_3'=2] {'rows_3'}, dimensions={0} | all-to-all | bytes 1024 | tf_op jit(solution)/shard_map/all_to_all | solution.py:20
  287.8 19.1 %all_to_all.67 = f32[64,1,64]{2,1,0:T(1,128)S(1)} all-to-all(f32[64,1,64]{2,1,0:T(1,128)S(1)} %broadcast_in_dim.28), channel_id=1, replica_groups=mesh['rows_0'=4,'rows_1'=4,'rows_2'=4,'rows_3'=2] {'rows_0','rows_1','ro..., dimensions={0} | all-to-all | bytes 32768 | tf_op jit(solution)/shard_map/all_to_all | solution.py:20
  307.0 1.8 multiply_add_fusion
  308.8 1.0 fusion.139
  309.8 1.7 fusion.22
  311.5 1.7 fusion.16
  313.6 9.9 %all_to_all.68 = f32[8,1,8192]{2,1,0:T(1,128)S(1)} all-to-all(f32[8,1,8192]{2,1,0:T(1,128)S(1)} %broadcast_in_dim.29), channel_id=1, replica_groups=mesh['rows_0'=4,'rows_1'=4,'rows_2'=4,'rows_3'=2] {'rows_2','rows_3'}, dimensions={0} | all-to-all | bytes 524288 | tf_op jit(solution)/shard_map/all_to_all | solution.py:20
  323.7 1.2 broadcast_in_dim.30
  324.9 3.6 all-to-all-start.9
  328.7 11.2 %all-to-all-done.9 = f32[16,1,8192]{2,1,0:T(1,128)S(1)} async-done(((f32[16,1,8192]{2,1,0:T(1,128)}), f32[16,1,8192]{2,1,0:T(1,128)S(1)}, u32[]{:S(2)}, u32[]{:S(2)}) %all-to-all-start.9) | async-done | bytes 524320 | tf_op jit(solution)/shard_map/all_to_all | solution.py:20
  340.7 8.8 %cholesky.20 = f32[96,96]{1,0:T(8,128)S(1)} custom-call(f32[96,96]{1,0:T(8,128)S(1)} %fusion.81), custom_call_target="Cholesky" | custom-call | tf_op jit(solution)/shard_map/jit(cholesky)/cholesky | solution.py:142
  350.8 7.4 %custom-call.8 = f32[1,96,96]{1,2,0:T(8,128)S(1)} custom-call(f32[1,96,96]{2,1,0:T(8,128)S(1)} %fusion.73), custom_call_target="InvertDiagBlocksLowerTriangular" | custom-call | tf_op jit(solution)/shard_map/jit(_solve_triangular)/triangular_solve | solution.py:144
  358.9 0.7 copy.85
  (117 shorter events, 10.2 us)
Async XLA Ops:
  1.5 27.9 %collective-permute-start = (f32[32,1024]{1,0:T(8,128)S(1)}, f32[32,1024]{1,0:T(8,128)S(1)}, u32[]{:S(2)}, u32[]{:S(2)}) collective-permute-start(f32[32,1024]{1,0:T(8,128)S(1)} %slice.114), channel_id=1, source_target_pairs={{1,0},{2,1},{3,2},{4,3},{5,4},{6,5},{7,6},{8,7},{9,8},{10,9},{11,1... | collective-permute-start | bytes 393224 | tf_op jit(solution)/shard_map/ppermute | solution.py:15
  26.3 3.2 copy-start
  28.8 21.5 %collective-permute-start.1 = (f32[32,1024]{1,0:T(8,128)S(1)}, f32[32,1024]{1,0:T(8,128)S(1)}, u32[]{:S(2)}, u32[]{:S(2)}) collective-permute-start(f32[32,1024]{1,0:T(8,128)S(1)} %bitcast.232), channel_id=1, source_target_pairs={{127,0},{0,1},{1,2},{2,3},{3,4},{4,5},{5,6},{6,7},{7,8},{8,9},{9,1... | collective-permute-start | bytes 393224 | tf_op jit(solution)/shard_map/ppermute | solution.py:15
  31.5 18.9 %copy-start.13 = (f32[4096]{0:T(1024)S(1)}, f32[4096]{0:T(1024)}, u32[]{:S(2)}) copy-start(f32[4096]{0:T(1024)} %param.13) | copy-start | bytes 49156
  50.3 1.0 copy-start.11
  50.7 34.0 %copy-start.1 = (f32[32,4096]{1,0:T(8,128)}, f32[32,4096]{1,0:T(8,128)S(1)}, u32[]{:S(2)}) copy-start(f32[32,4096]{1,0:T(8,128)S(1)} %get-tuple-element.22) | copy-start | bytes 1572868
  50.7 1.7 copy-start.8
  103.9 5.3 %collective-permute-start.2 = (f32[32,1024]{1,0:T(8,128)S(1)}, f32[32,1024]{1,0:T(8,128)S(1)}, u32[]{:S(2)}, u32[]{:S(2)}) collective-permute-start(f32[32,1024]{1,0:T(8,128)S(1)} %slice.145), channel_id=1, source_target_pairs={{1,0},{2,1},{3,2},{4,3},{5,4},{6,5},{7,6},{8,7},{9,8},{10,9},{11,1... | collective-permute-start | bytes 393224 | tf_op jit(solution)/shard_map/ppermute | solution.py:15
  109.1 23.0 %collective-permute-start.3 = (f32[32,1024]{1,0:T(8,128)}, f32[32,1024]{1,0:T(8,128)}, u32[]{:S(2)}, u32[]{:S(2)}) collective-permute-start(f32[32,1024]{1,0:T(8,128)} %bitcast.104), channel_id=1, source_target_pairs={{127,0},{0,1},{1,2},{2,3},{3,4},{4,5},{5,6},{6,7},{7,8},{8,9},{9,1... | collective-permute-start | bytes 393224 | tf_op jit(solution)/shard_map/ppermute | solution.py:15
  113.2 18.9 %copy-start.6 = (f32[4,8,16,256]{3,1,2,0:T(8,128)S(1)}, f32[4,8,16,256]{3,1,2,0:T(8,128)}, u32[]{:S(2)}) copy-start(f32[4,8,16,256]{3,1,2,0:T(8,128)} %copy.129) | copy-start | bytes 1572868
  177.3 5.5 %collective-permute-start.4 = (f32[32,1024]{1,0:T(8,128)S(1)}, f32[32,1024]{1,0:T(8,128)S(1)}, u32[]{:S(2)}, u32[]{:S(2)}) collective-permute-start(f32[32,1024]{1,0:T(8,128)S(1)} %slice.148), channel_id=1, source_target_pairs={{1,0},{2,1},{3,2},{4,3},{5,4},{6,5},{7,6},{8,7},{9,8},{10,9},{11,1... | collective-permute-start | bytes 393224 | tf_op jit(solution)/shard_map/ppermute | solution.py:15
  182.4 25.2 %collective-permute-start.5 = (f32[32,1024]{1,0:T(8,128)}, f32[32,1024]{1,0:T(8,128)S(1)}, u32[]{:S(2)}, u32[]{:S(2)}) collective-permute-start(f32[32,1024]{1,0:T(8,128)} %bitcast.108), channel_id=1, source_target_pairs={{127,0},{0,1},{1,2},{2,3},{3,4},{4,5},{5,6},{6,7},{7,8},{8,9},{9,1... | collective-permute-start | bytes 393224 | tf_op jit(solution)/shard_map/ppermute | solution.py:15
  188.7 18.9 %copy-start.7 = (f32[4,8,16,256]{3,1,2,0:T(8,128)S(1)}, f32[4,8,16,256]{3,1,2,0:T(8,128)}, u32[]{:S(2)}) copy-start(f32[4,8,16,256]{3,1,2,0:T(8,128)} %copy.131) | copy-start | bytes 1572868
  232.8 0.8 copy-start.3
  252.8 5.3 %collective-permute-start.6 = (f32[32,1024]{1,0:T(8,128)S(1)}, f32[32,1024]{1,0:T(8,128)S(1)}, u32[]{:S(2)}, u32[]{:S(2)}) collective-permute-start(f32[32,1024]{1,0:T(8,128)S(1)} %slice.151), channel_id=1, source_target_pairs={{1,0},{2,1},{3,2},{4,3},{5,4},{6,5},{7,6},{8,7},{9,8},{10,9},{11,1... | collective-permute-start | bytes 393224 | tf_op jit(solution)/shard_map/ppermute | solution.py:15
  257.8 25.1 %collective-permute-start.7 = (f32[32,1024]{1,0:T(8,128)}, f32[32,1024]{1,0:T(8,128)S(1)}, u32[]{:S(2)}, u32[]{:S(2)}) collective-permute-start(f32[32,1024]{1,0:T(8,128)} %bitcast.112), channel_id=1, source_target_pairs={{127,0},{0,1},{1,2},{2,3},{3,4},{4,5},{5,6},{6,7},{7,8},{8,9},{9,1... | collective-permute-start | bytes 393224 | tf_op jit(solution)/shard_map/ppermute | solution.py:15
  264.0 18.9 %copy-start.4 = (f32[32,4096]{1,0:T(8,128)S(1)}, f32[32,4096]{1,0:T(8,128)}, u32[]{:S(2)}) copy-start(f32[32,4096]{1,0:T(8,128)} %copy-done.3) | copy-start | bytes 1572868
  264.0 18.9 %copy-start.5 = (f32[4,8,16,256]{3,1,2,0:T(8,128)S(1)}, f32[4,8,16,256]{3,1,2,0:T(8,128)}, u32[]{:S(2)}) copy-start(f32[4,8,16,256]{3,1,2,0:T(8,128)} %copy.133) | copy-start | bytes 1572868
  307.0 2.8 copy-start.2
  307.0 2.8 copy-start.9
  308.8 2.7 copy-start.10
  308.8 2.7 copy-start.12
  324.9 15.0 %all-to-all-start.9 = ((f32[16,1,8192]{2,1,0:T(1,128)}), f32[16,1,8192]{2,1,0:T(1,128)S(1)}, u32[]{:S(2)}, u32[]{:S(2)}) async-start(f32[16,1,8192]{2,1,0:T(1,128)} %broadcast_in_dim.30), calls=%async_computation.9 | async-start | bytes 1048576 | tf_op jit(solution)/shard_map/all_to_all | solution.py:20
where the time goes:
time: 367 us; the launch traced here: 360 us
  matrix products  172 us (47%)
  blocking collectives  108 us (29%)
  other arithmetic  32.2 us (9%)
  local copies, waits for them, and re-layouts  19 us (5%)
  starting transfers between devices  15.3 us (4%)
  waiting for transfers between devices  11.2 us (3%)
    all_to_all x9, blocking collectives, copy_for_each(): lax.all_to_all(jnp.broadcast_to(shard[None], (count, *shard.shape)), axis...  108 us
    dot_general x4, matrix products, padded_apply(): jnp.einsum('bsij,kbsj->kbi', tiles, picked, precision=lax.Precision.HIGHEST)  75.2 us
    dot_general x4, matrix products, padded_apply(): jnp.einsum('kbi,bsij->kbsj', source, tiles, precision=lax.Precision.HIGHEST)  52.8 us
    dot_general x3, matrix products, local(): jnp.einsum('bij,kbj->kbi', precond, shaped, precision=lax.Precision.HIGHEST)  18.2 us
    ppermute x8, starting transfers between devices, shifted(): return lax.ppermute(block, axis, route)  11.7 us
    all_to_all x1, waiting for transfers between devices, copy_for_each(): lax.all_to_all(jnp.broadcast_to(shard[None], (count, *shard.shape)), axis...  11.2 us
    dot_general x4, matrix products, padded_apply(): jnp.einsum('bse,kbsj->kej', one_hot, moved, precision=lax.Precision.HIGHEST)  9.72 us
    dot_general x4, matrix products, padded_apply(): jnp.einsum('bse,kej->kbsj', one_hot, extended, precision=lax.Precision.HI...  9.59 us
  transfers between devices with their start and end apart: 9, of which 1 were waited for; matrix products, arithmetic and copies ran while one was open for 35% of the time, Pallas kernels for 0%

commit v1 on v0

v1 whole, which is shorter than its diff:
```python
import jax
import jax.numpy as jnp
from jax import lax
from jax.experimental import pallas as pl
from jax.experimental.pallas import tpu as pltpu
from jax.sharding import PartitionSpec as P

MESH = pl.DeviceIdType.MESH
F32 = jnp.float32
BF16 = jnp.bfloat16
HB = 4
ITERS = 3
LOW = 8
SLOTS = 4
STAGES = 4


def split(x):
    high = x.astype(BF16)
    return high, (x - high.astype(F32)).astype(BF16)


def mm(a, b):
    return jnp.dot(a, b, preferred_element_type=F32)


def mmt(a, b):
    return lax.dot_general(a, b, (((1,), (1,)), ((), ())), preferred_element_type=F32)


def kernel(
    n_dev, rows, kvec, bs,
    cols, live, blocks, onsite, precond, vec, pvec, pimg,
    corr, mats,
    stage, bh, bl, ph, plo, offs,
    fv, fpv, fpi, fim, fr, fu, fhu, fa, fz, fc, fh, zs, acc, qb, sb,
    zhalo, inc, spill, red1, red2, gram, parts, big1, big2, fin,
    stage_sem, load_sem, out_sem, zs_sem, zr_sem, ss_sem, sr_sem,
    r1s, r1r, r2s, r2r, b1s, b1r, b2s, b2r, b3s, b3r,
):
    me = lax.axis_index("rows")
    low = lax.rem(me, LOW)
    high = lax.div(me, LOW)
    n_high = n_dev // LOW
    total = n_dev * rows
    first = me * rows
    right = lax.rem(me + 1, n_dev)
    left = lax.rem(me + n_dev - 1, n_dev)
    edge = rows - HB
    order = list(range(edge, rows)) + list(range(edge))

    def load_field(src, dst, sem):
        for b in range(rows):
            pltpu.make_async_copy(src.at[:, pl.ds(b * bs, bs)], dst.at[b], sem).start()

    def load_wait(dst, sem):
        pltpu.make_async_copy(dst, dst, sem).wait()

    n_chunks = rows + rows // SLOTS

    def chunk(i):
        slot = i % STAGES
        if i < rows:
            src = blocks.at[order[i]]
        else:
            src = precond.at[pl.ds((i - rows) * SLOTS, SLOTS)]
        return pltpu.make_async_copy(src, stage.at[slot], stage_sem.at[slot])

    load_field(vec, fv, load_sem.at[0])
    for i in range(STAGES):
        chunk(i).start()

    barrier = pltpu.get_barrier_semaphore()
    peers = [left, right]
    peers += [high * LOW + lax.rem(low + j, LOW) for j in range(1, LOW)]
    peers += [lax.rem(high + j, n_high) * LOW + low for j in range(1, n_high)]
    for peer in peers:
        pl.semaphore_signal(barrier, inc=1, device_id=(peer,), device_id_type=MESH)
    pl.semaphore_wait(barrier, len(peers))

    def rcopy(src, dst, s_sem, r_sem, to):
        return pltpu.make_async_remote_copy(
            src_ref=src, dst_ref=dst, send_sem=s_sem, recv_sem=r_sem,
            device_id=(to,), device_id_type=MESH,
        )

    def z_copy(n, field):
        return rcopy(field.at[pl.ds(0, HB)], zhalo.at[n], zs_sem.at[n], zr_sem.at[n], left)

    def spill_copy(n):
        return rcopy(spill.at[n], inc.at[n], ss_sem.at[n], sr_sem.at[n], right)

    def low_copy(i, j):
        to = high * LOW + lax.rem(low + j, LOW)
        return rcopy(red1.at[i, low], red1.at[i, low], r1s.at[i, j], r1r.at[i, low], to)

    def low_in(i, j):
        frm = lax.rem(low + j, LOW)
        return rcopy(red1.at[i, frm], red1.at[i, frm], r1s.at[i, j], r1r.at[i, frm], left)

    def high_copy(i, j):
        to = lax.rem(high + j, n_high) * LOW + low
        return rcopy(red2.at[i, high], red2.at[i, high], r2s.at[i, j], r2r.at[i, high], to)

    def high_in(i, j):
        frm = lax.rem(high + j, n_high)
        return rcopy(red2.at[i, frm], red2.at[i, frm], r2s.at[i, j], r2r.at[i, frm], left)

    lane = lax.broadcasted_iota(jnp.int32, (8, 128), 1)
    groups = kvec // 8

    def pack(a, b):
        tile = jnp.zeros((8, 128), F32)
        for g in range(groups):
            tile = tile + jnp.where(lane == g, a[8 * g:8 * g + 8], 0.0)
            tile = tile + jnp.where(lane == groups + g, b[8 * g:8 * g + 8], 0.0)
        return tile

    def unpack(tile):
        out = []
        for base in (0, groups):
            out.append(jnp.concatenate(
                [jnp.sum(jnp.where(lane == base + g, tile, 0.0), axis=1, keepdims=True) for g in range(groups)],
                axis=0,
            ))
        return out

    def red_start(i, a, b):
        red1[i, low] = pack(a, b)
        for j in range(1, LOW):
            low_copy(i, j).start()

    def red_mid(i):
        for j in range(1, LOW):
            low_in(i, j).wait_recv()
        tile = red1[i, 0]
        for l in range(1, LOW):
            tile = tile + red1[i, l]
        red2[i, high] = tile
        for j in range(1, n_high):
            high_copy(i, j).start()

    def red_end(i):
        for j in range(1, n_high):
            high_in(i, j).wait_recv()
        tile = red2[i, 0]
        for l in range(1, n_high):
            tile = tile + red2[i, l]
        for j in range(1, LOW):
            low_copy(i, j).wait_send()
        for j in range(1, n_high):
            high_copy(i, j).wait_send()
        return unpack(tile)

    def put_split(b, z):
        zh, zl = split(z)
        zs[b, 0:kvec, :] = zh
        zs[b, kvec:2 * kvec, :] = zl

    def onto(b):
        zb = zs[b]
        zh = zb[0:kvec]
        sums = [None] * (HB + 1)
        for s in range(SLOTS):
            part = mm(zb, bh[b * SLOTS + s])
            moved = part[0:kvec] + part[kvec:] + mm(zh, bl[b * SLOTS + s])
            off = offs[b * SLOTS + s]
            for o in range(HB + 1):
                term = jnp.where(off == o, 1.0, 0.0) * moved
                sums[o] = term if sums[o] is None else sums[o] + term
        for o in range(HB + 1):
            acc[b + o] = acc[b + o] + sums[o]

    def across(b):
        out = None
        for s in range(SLOTS):
            zc = zs[b + offs[b * SLOTS + s]]
            part = mmt(zc, bh[b * SLOTS + s])
            term = part[0:kvec] + part[kvec:] + mmt(zc[0:kvec], bl[b * SLOTS + s])
            out = term if out is None else out + term
        acc[b] = acc[b] + out

    def halo_in(n):
        z_copy(n, fv).wait_recv()
        for t in range(HB):
            put_split(rows + t, zhalo[n, t])

    def send_spill(n):
        for t in range(HB):
            spill[n, t] = acc[rows + t]
        spill_copy(n).start()

    def take_in(n):
        spill_copy(n).wait_recv()
        for t in range(HB):
            acc[t] = acc[t] + inc[n, t]

    def diag(b, z):
        acc[b] = onsite[b] * z

    def clear_tail():
        for t in range(HB):
            acc[rows + t] = jnp.zeros((kvec, bs), F32)

    load_wait(fv, load_sem.at[0])
    z_copy(0, fv).start()
    load_field(pvec, fpv, load_sem.at[1])
    load_field(pimg, fpi, load_sem.at[2])

    def prepare(b, c):
        z = fv[b]
        put_split(b, z)
        diag(b, z)
        return c

    lax.fori_loop(0, rows, prepare, 0)
    clear_tail()

    def take_chunk(i):
        chunk(i).wait()
        slot = i % STAGES
        if i < rows:
            b = order[i]
            for s in range(SLOTS):
                off = lax.rem(cols[b, s] - first - b + 2 * total, total)
                offs[b * SLOTS + s] = jnp.minimum(off, HB)
                alive = jnp.where(s < live[b], 1.0, 0.0)

                def piece(p, c):
                    at = pl.ds(pl.multiple_of(p * 64, 64), 64)
                    xh, xl = split(stage[slot, s, at, :] * alive)
                    bh[b * SLOTS + s, at, :] = xh
                    bl[b * SLOTS + s, at, :] = xl
                    return c

                lax.fori_loop(0, bs // 64, piece, 0)
        else:
            for s in range(SLOTS):
                def piece(p, c):
                    at = pl.ds(pl.multiple_of(p * 64, 64), 64)
                    xh, xl = split(stage[slot, s, at, :])
                    ph[(i - rows) * SLOTS + s, at, :] = xh
                    plo[(i - rows) * SLOTS + s, at, :] = xl
                    return c

                lax.fori_loop(0, bs // 64, piece, 0)
        if i + STAGES < n_chunks:
            chunk(i + STAGES).start()

    for i in range(HB):
        take_chunk(i)
        onto(order[i])
    send_spill(0)
    for i in range(HB, rows):
        take_chunk(i)
        onto(order[i])
        across(order[i])
    halo_in(0)
    for b in range(edge, rows):
        across(b)
    take_in(0)

    zero = jnp.zeros((kvec, bs), F32)

    def first_sums(b, c):
        x, im = fv[b], acc[b]
        fim[b] = im
        return c[0] + x * im, c[1] + x * x

    num, den = lax.fori_loop(0, rows, first_sums, (zero, zero))
    total_of = lambda x: jnp.sum(x, axis=1, keepdims=True)
    red_start(0, total_of(num), total_of(den))
    for i in range(rows, n_chunks):
        take_chunk(i)
    red_mid(0)
    num, den = red_end(0)
    q = num / den
    qb[...] = jnp.broadcast_to(q, (kvec, bs))

    def first_rest(b, c):
        fr[b] = qb[...] * fv[b] - fim[b]
        return c

    lax.fori_loop(0, rows, first_rest, 0)

    def precondition(field, b):
        dh, dl = split(field[b])
        both = jnp.concatenate([dh, dl], axis=0)
        part = mmt(both, ph[b])
        z = part[0:kvec] + part[kvec:] + mmt(dh, plo[b])
        fz[b] = z
        put_split(b, z)
        diag(b, z)

    for k in range(ITERS):
        n = k + 1
        field = fr if k == 0 else fa
        for b in range(HB):
            precondition(field, b)
        z_copy(n, fz).start()
        clear_tail()
        for b in range(edge, rows):
            precondition(field, b)
        for b in range(edge, rows):
            onto(b)
        send_spill(n)

        def interior(g, c, field=field):
            for t in range(4):
                precondition(field, 4 + 4 * g + t)
            return c

        lax.fori_loop(0, (edge - HB) // 4, interior, 0)
        if k > 0:
            red_mid(k)

        def body(g, c):
            for t in range(4):
                onto(4 * g + t)
            for t in range(4):
                across(4 * g + t)
            return c

        lax.fori_loop(0, edge // 4, body, 0)
        halo_in(n)
        for b in range(edge, rows):
            across(b)
        take_in(n)
        z_copy(n, fz).wait_send()
        if k > 0:
            cross, own = red_end(k)
            step = cross / (own + 1.0)
            sb[...] = jnp.broadcast_to(step, (kvec, bs))

        def update(b, c, k=k):
            z, hz = fz[b], acc[b]
            m = hz - qb[...] * z
            if k == 0:
                r = fr[b]
                a = m
                fu[b] = z
                fhu[b] = hz
            else:
                s = sb[...]
                u, hu, a = fu[b], fhu[b], fa[b]
                r = fr[b] - s * a
                fr[b] = r
                if k == 1:
                    fc[b] = s * u
                    fh[b] = s * hu
                else:
                    fc[b] = fc[b] + s * u
                    fh[b] = fh[b] + s * hu
                a = a - s * m
                fu[b] = u - s * z
                fhu[b] = hu - s * hz
            fa[b] = a
            return c[0] + a * r, c[1] + a * a

        cross, own = lax.fori_loop(0, rows, update, (zero, zero))
        if k + 1 < ITERS:
            red_start(k + 1, total_of(cross), total_of(own))

    load_wait(fpv, load_sem.at[1])
    load_wait(fpi, load_sem.at[2])
    gram[...] = jnp.zeros_like(gram)

    def products(b, c):
        xh, xl = split(jnp.concatenate([fv[b], fpv[b], fc[b], fu[b]], axis=0))
        yh, yl = split(jnp.concatenate([fim[b], fpi[b], fh[b], fhu[b]], axis=0))
        part = mmt(jnp.concatenate([xh, xl], axis=0), jnp.concatenate([xh, yh], axis=0))
        m = xh.shape[0]
        gram[...] = gram[...] + (part[0:m] + part[m:] + mmt(xh, jnp.concatenate([xl, yl], axis=0)))
        return c

    lax.fori_loop(0, rows, products, 0)
    wide = lax.broadcasted_iota(jnp.int32, (kvec, 128), 1)
    for p in range(4):
        at = pl.ds(p * kvec, kvec)
        g = gram[at, 0:128]
        if p == 0:
            g = jnp.where(wide == 96, total_of(cross), jnp.where(wide == 97, total_of(own), g))
        parts[p] = g
        parts[4 + p] = gram[at, 128:256]

    def big1_copy(j):
        to = lax.rem(low + j, LOW)
        return rcopy(parts.at[to], big1.at[low], b1s.at[j], b1r.at[low], high * LOW + to)

    def big1_in(j):
        frm = lax.rem(low + j, LOW)
        return rcopy(parts.at[frm], big1.at[frm], b1s.at[j], b1r.at[frm], left)

    def big2_copy(j):
        to = lax.rem(high + j, n_high) * LOW + low
        return rcopy(big2.at[high], big2.at[high], b2s.at[j], b2r.at[high], to)

    def big2_in(j):
        frm = lax.rem(high + j, n_high)
        return rcopy(big2.at[frm], big2.at[frm], b2s.at[j], b2r.at[frm], left)

    def fin_copy(j):
        to = high * LOW + lax.rem(low + j, LOW)
        return rcopy(fin.at[low], fin.at[low], b3s.at[j], b3r.at[low], to)

    def fin_in(j):
        frm = lax.rem(low + j, LOW)
        return rcopy(fin.at[frm], fin.at[frm], b3s.at[j], b3r.at[frm], left)

    for j in range(1, LOW):
        big1_copy(j).start()
    big1[low] = parts[low]
    for j in range(1, LOW):
        big1_in(j).wait_recv()
    tile = big1[0]
    for l in range(1, LOW):
        tile = tile + big1[l]
    big2[high] = tile
    for j in range(1, n_high):
        big2_copy(j).start()
    for j in range(1, n_high):
        big2_in(j).wait_recv()
    tile = big2[0]
    for l in range(1, n_high):
        tile = tile + big2[l]
    fin[low] = tile
    for j in range(1, LOW):
        fin_copy(j).start()
    for j in range(1, LOW):
        fin_in(j).wait_recv()

    head = fin[0]
    step = head[:, 96:97] / (head[:, 97:98] + 1.0)
    sb[...] = jnp.broadcast_to(step, (kvec, bs))

    def finish(b, c):
        fc[b] = fc[b] + sb[...] * fu[b]
        return c

    lax.fori_loop(0, rows, finish, 0)
    for b in range(rows):
        pltpu.make_async_copy(fc.at[b], corr.at[:, pl.ds(b * bs, bs)], out_sem).start()
    for p in range(8):
        mats[p] = fin[p]
    pltpu.make_async_copy(fc, fc, out_sem).wait()

    for j in range(1, LOW):
        big1_copy(j).wait_send()
        fin_copy(j).wait_send()
    for j in range(1, n_high):
        big2_copy(j).wait_send()
    z_copy(0, fv).wait_send()
    for n in range(ITERS + 1):
        spill_copy(n).wait_send()


def local(n_dev, blocks, block_cols, live_counts, onsite_energy, precond, vectors, prev_vectors, prev_image):
    rows, slots, bs = blocks.shape[0], blocks.shape[1], blocks.shape[2]
    kvec = vectors.shape[0]
    n_high = n_dev // LOW
    field = pltpu.VMEM((rows, kvec, bs), F32)
    dma = pltpu.SemaphoreType.DMA
    hbm = pl.BlockSpec(memory_space=pl.ANY)
    smem = pl.BlockSpec(memory_space=pltpu.SMEM)
    vmem = pl.BlockSpec(memory_space=pltpu.VMEM)

    def run(*args):
        return kernel(n_dev, rows, kvec, bs, *args)

    correction, mats = pl.pallas_call(
        run,
        out_shape=(
            jax.ShapeDtypeStruct(vectors.shape, F32),
            jax.ShapeDtypeStruct((8, kvec, 128), F32),
        ),
        in_specs=[smem, smem, hbm, vmem, hbm, hbm, hbm, hbm],
        out_specs=(hbm, vmem),
        scratch_shapes=[
            pltpu.VMEM((STAGES, slots, bs, bs), F32),
            pltpu.VMEM((rows * slots, bs, bs), BF16),
            pltpu.VMEM((rows * slots, bs, bs), BF16),
            pltpu.VMEM((rows, bs, bs), BF16),
            pltpu.VMEM((rows, bs, bs), BF16),
            pltpu.SMEM((rows * slots,), jnp.int32),
            field, field, field, field, field, field, field, field, field, field, field,
            pltpu.VMEM((rows + HB, 2 * kvec, bs), BF16),
            pltpu.VMEM((rows + HB, kvec, bs), F32),
            pltpu.VMEM((kvec, bs), F32),
            pltpu.VMEM((kvec, bs), F32),
            pltpu.VMEM((ITERS + 1, HB, kvec, bs), F32),
            pltpu.VMEM((ITERS + 1, HB, kvec, bs), F32),
            pltpu.VMEM((ITERS + 1, HB, kvec, bs), F32),
            pltpu.VMEM((ITERS, LOW, 8, 128), F32),
            pltpu.VMEM((ITERS, n_high, 8, 128), F32),
            pltpu.VMEM((4 * kvec, 256), F32),
            pltpu.VMEM((8, kvec, 128), F32),
            pltpu.VMEM((LOW, kvec, 128), F32),
            pltpu.VMEM((n_high, kvec, 128), F32),
            pltpu.VMEM((8, kvec, 128), F32),
            dma((STAGES,)), dma((3,)), dma,
            dma((ITERS + 1,)), dma((ITERS + 1,)), dma((ITERS + 1,)), dma((ITERS + 1,)),
            dma((ITERS, LOW)), dma((ITERS, LOW)), dma((ITERS, n_high)), dma((ITERS, n_high)),
            dma((LOW,)), dma((LOW,)), dma((n_high,)), dma((n_high,)), dma((LOW,)), dma((LOW,)),
        ],
        compiler_params=pltpu.CompilerParams(
            collective_id=0, has_side_effects=True, vmem_limit_bytes=60 * 1024 * 1024
        ),
    )(block_cols, live_counts, blocks, onsite_energy.reshape(rows, 1, bs), precond, vectors, prev_vectors, prev_image)
    gram = mats[0:4].reshape(4 * kvec, 128)
    proj = mats[4:8].reshape(4 * kvec, 128)
    step = gram[0:kvec, 96] / (gram[0:kvec, 97] + 1.0)

    def combine(x):
        x = jnp.concatenate([x[0:64], x[64:96] + step[:, None] * x[96:128]], axis=0)
        return jnp.concatenate([x[:, 0:64], x[:, 64:96] + step[None, :] * x[:, 96:128]], axis=1)

    lower = combine(gram)
    tail = lower[64:96]
    gram_matrix = jnp.concatenate(
        [jnp.concatenate([lower[0:64, 0:64], tail[:, 0:64].T], axis=1), tail], axis=0
    )
    projected = combine(proj)
    gram_matrix = gram_matrix + jnp.eye(gram_matrix.shape[0], dtype=F32)
    factor = jnp.linalg.cholesky(gram_matrix)
    half_way = jax.scipy.linalg.solve_triangular(factor, projected, lower=True)
    reduced = jax.scipy.linalg.solve_triangular(factor, half_way.T, lower=True).T
    return correction, reduced


def solution(mesh):
    n_dev = mesh.shape["rows"]

    def step(*args):
        return local(n_dev, *args)

    return jax.shard_map(
        step,
        mesh=mesh,
        in_specs=(
            P("rows", None, None, None), P("rows", None), P("rows"), P("rows"),
            P("rows", None, None), P(None, "rows"), P(None, "rows"), P(None, "rows"),
        ),
        out_specs=(P(None, "rows"), P()),
        check_vma=False,
    )
```

time: 367 us -> 119 us (0.32); the launches traced: 360 us -> 118 us
  matrix products: 172 us -> 0.55 us
  blocking collectives: 108 us -> 0 us
  Pallas kernels: 0 us -> 92.1 us
  starting transfers between devices: 15.3 us -> 0 us
  other arithmetic: 32.2 us -> 18.6 us
  local copies, waits for them, and re-layouts: 19 us -> 5.95 us
  waiting for transfers between devices: 11.2 us -> 0 us
    dot_general x24 -> x0, matrix products: 172 us -> none  [the longest x4 75.2 us: padded_apply(): jnp.einsum('bsij,kbsj->kbi', tiles, picked, precision=lax.Precision.HIGHEST)]
    all_to_all x9 -> x0, blocking collectives: 108 us -> none  [copy_for_each(): lax.all_to_all(jnp.broadcast_to(shard[None], (count, *shard.shape)), axis...]
    pallas_call x0 -> x1, Pallas kernels: none -> 92.1 us  [local(): pl.pallas_call(run, out_shape=(jax.ShapeDtypeStruct(vectors.shape, F32),...]
    ppermute x8 -> x0, starting transfers between devices: 11.7 us -> none  [shifted(): return lax.ppermute(block, axis, route)]
    all_to_all x1 -> x0, waiting for transfers between devices: 11.2 us -> none  [copy_for_each(): lax.all_to_all(jnp.broadcast_to(shard[None], (count, *shard.shape)), axis...]
    reshape x20 -> x0, local copies, waits for them, and re-layouts: 6.37 us -> none  [the longest x4 5.46 us: operate(): jnp.concatenate([field, right_rows], axis=1)]
    reduce_sum x14 -> x0, other arithmetic: 5.72 us -> none  [the longest x3 4.19 us: local(): jnp.sum(applied * remainder, axis=1)]
    unnamed x38 -> x5, local copies, waits for them, and re-layouts: 9.05 us -> 4.09 us
  transfers between devices with their start and end apart: 9 -> 0, of which waited for: 1 -> 0; matrix products, arithmetic and copies ran while one was open for 35% -> 0% of each run, Pallas kernels for 0% -> 0%
where the time goes in v1:
time: 119 us; the launch traced here: 118 us
  Pallas kernels  92.1 us (77%)
  other arithmetic  18.6 us (16%)
  local copies, waits for them, and re-layouts  5.95 us (5%)
    pallas_call x1, Pallas kernels, local(): pl.pallas_call(run, out_shape=(jax.ShapeDtypeStruct(vectors.shape, F32),...  92.1 us
    another operation x3, other arithmetic, local(): factor = jnp.linalg.cholesky(gram_matrix)  9.45 us
    another operation x2, other arithmetic, local(): jax.scipy.linalg.solve_triangular(factor, half_way.T, lower=True)  8.01 us
    unnamed x5, local copies, waits for them, and re-layouts  4.09 us

profile of v1, /device:TPU:0, one launch (start us, length us, event | category | flops | bytes accessed | tf_op | source)
XLA Modules:
  0.0 117.8 jit_solution(114064703729078052)
XLA Ops:
  0.6 1.4 %copy.10.args_0_ = s32[16,4]{1,0:T(8,128)} copy(s32[16,4]{0,1:T(4,128)} %param.11) | data formatting | bytes 512 | tf_op args[1]
  2.0 92.1 %shard_map.95 = (f32[32,4096]{1,0:T(8,128)}, f32[8,32,128]{2,1,0:T(8,128)}) custom-call(s32[16,4]{1,0:T(8,128)} %copy.10.args_0_, s32[16]{0:T(128)} %args_1_.4, f32[16,4,256,256]{3,2,1,0:T(8,128)} %args_2_.4, f32[16,1,256]{2,1,0:T(1,128)} %bitcast.45, f32[16,256,256]{2,1,0:T(8,128)} %args_4_.4, f32[32,4096]{1,0:T(8,128)} %args_5_.4, f32[32,4096]{1,0:T(8,128)} %args_6_.4, ...), custom_call_target="tpu_custom_call" | custom-call | tf_op jit(solution)/shard_map/pallas_call | solution.py:470
  94.1 0.8 slice.100
  94.9 0.1 fusion.22
  95.0 0.1 copy.16
  95.1 0.1 copy.17
  95.1 0.9 fusion.18
  96.0 0.8 fusion.21
  96.8 0.1 fusion.4
  96.9 0.1 copy.13
  97.0 0.1 fusion.9
  97.1 0.1 copy.14
  97.2 8.8 %cholesky.20 = f32[96,96]{1,0:T(8,128)S(1)} custom-call(f32[96,96]{1,0:T(8,128)S(1)} %fusion.16), custom_call_target="Cholesky" | custom-call | tf_op jit(solution)/shard_map/jit(cholesky)/cholesky | solution.py:524
  106.0 0.6 compare_reduce_fusion
  106.7 0.7 fusion.6
  107.3 7.4 %custom-call.8 = f32[1,96,96]{1,2,0:T(8,128)S(1)} custom-call(f32[1,96,96]{2,1,0:T(8,128)S(1)} %fusion.6), custom_call_target="InvertDiagBlocksLowerTriangular" | custom-call | tf_op jit(solution)/shard_map/jit(_solve_triangular)/triangular_solve | solution.py:526
  114.7 0.3 convolution_bitcast_fusion.1
  115.0 0.3 convolution_bitcast_fusion
  115.3 0.7 copy.15
  116.0 1.9 %copy.19 = f32[32,4096]{1,0:T(8,128)} copy(f32[32,4096]{1,0:T(8,128)} %get-tuple-element.21) | data formatting | bytes 1048576
  (5 shorter events, 0.1 us)

commit v2 on v1

--- a/solution.py
+++ b/solution.py
@@ -28,13 +28,72 @@
     return lax.dot_general(a, b, (((1,), (1,)), ((), ())), preferred_element_type=F32)
 
 
+def reduce_basis(gram, proj, step, aug, kvec):
+    width = 128
+    size = 3 * kvec
+    lane = lax.broadcasted_iota(jnp.int32, (kvec, width), 1)
+    row = lax.broadcasted_iota(jnp.int32, (kvec, width), 0)
+    step_row = jnp.sum(jnp.where(lane == row + size, step, 0.0), axis=0, keepdims=True)
+
+    def fold(x):
+        n = x.shape[0]
+        at = lax.broadcasted_iota(jnp.int32, (n, width), 1)
+        moved = pltpu.roll(x * step_row, width - kvec, 1)
+        return jnp.where(at < 2 * kvec, x, jnp.where(at < size, x + moved, 0.0))
+
+    tail = fold(gram[2] + step * gram[3])
+    above = jnp.concatenate([jnp.zeros((2 * kvec, width), F32), tail, jnp.zeros((kvec, width), F32)], axis=0).T
+    for g in range(2):
+        a = jnp.where(lane < 2 * kvec, gram[g], above[g * kvec:(g + 1) * kvec])
+        aug[g * kvec:(g + 1) * kvec, 0:width] = a + jnp.where(lane == row + g * kvec, 1.0, 0.0)
+    aug[2 * kvec:size, 0:width] = tail + jnp.where(lane == row + 2 * kvec, 1.0, 0.0)
+    for g in range(3):
+        aug[g * kvec:(g + 1) * kvec, width:2 * width] = jnp.where(lane == row + g * kvec, 1.0, 0.0)
+    x = jnp.concatenate([fold(proj[0]), fold(proj[1]), fold(proj[2] + step * proj[3]), jnp.zeros((kvec, width), F32)], axis=0)
+
+    sub = lax.broadcasted_iota(jnp.int32, (8, width), 0)
+    for top in range(0, size, 8):
+        n = size - top
+        cols = [jnp.broadcast_to(aug[top:size, top + c:top + c + 1], (n, width)) for c in range(8)]
+        pivot_rows = aug[top:top + 8, :]
+        facs = []
+        for j in range(8):
+            f = cols[j] * (1.0 / cols[j][j:j + 1, :])
+            head = jnp.where(sub > j, f[0:8], 0.0)
+            facs.append(f)
+            for c in range(j + 1, 8):
+                pr = cols[c][j:j + 1, :]
+                new_head = cols[c][0:8] - head * pr
+                cols[c] = new_head if n == 8 else jnp.concatenate([new_head, cols[c][8:] - f[8:] * pr], axis=0)
+            both = jnp.concatenate([head, head], axis=1)
+            pivot_rows = pivot_rows - both * pivot_rows[j:j + 1, :]
+        aug[top:top + 8, :] = pivot_rows
+        for r in range(top + 8, size, 8):
+            block = aug[r:r + 8, :]
+            for j in range(8):
+                f = facs[j][r - top:r - top + 8]
+                block = block - jnp.concatenate([f, f], axis=1) * pivot_rows[j:j + 1, :]
+            aug[r:r + 8, :] = block
+
+    at = lax.broadcasted_iota(jnp.int32, (size, width), 1)
+    diagonal = jnp.where(at == lax.broadcasted_iota(jnp.int32, (size, width), 0), aug[:, 0:width], 0.0)
+    by_row = lax.rsqrt(jnp.sum(diagonal, axis=1, keepdims=True))
+    by_col = jnp.sum(diagonal, axis=0, keepdims=True)
+    by_col = jnp.where(at[0:1] < size, lax.rsqrt(jnp.where(at[0:1] < size, by_col, 1.0)), 0.0)
+    w = aug[:, width:2 * width]
+    w_full = jnp.concatenate([w, jnp.zeros((kvec, width), F32)], axis=0)
+    half = jnp.dot(w, x, precision=lax.Precision.HIGHEST, preferred_element_type=F32)
+    full = lax.dot_general(half, w_full, (((1,), (1,)), ((), ())), precision=lax.Precision.HIGHEST, preferred_element_type=F32)
+    return full * by_row * by_col
+
+
 def kernel(
     n_dev, rows, kvec, bs,
     cols, live, blocks, onsite, precond, vec, pvec, pimg,
     corr, mats,
     stage, bh, bl, ph, plo, offs,
     fv, fpv, fpi, fim, fr, fu, fhu, fa, fz, fc, fh, zs, acc, qb, sb,
-    zhalo, inc, spill, red1, red2, gram, parts, big1, big2, fin,
+    zhalo, inc, spill, red1, red2, gram, parts, big1, big2, fin, aug,
     stage_sem, load_sem, out_sem, zs_sem, zr_sem, ss_sem, sr_sem,
     r1s, r1r, r2s, r2r, b1s, b1r, b2s, b2r, b3s, b3r,
 ):
@@ -440,8 +499,7 @@
     lax.fori_loop(0, rows, finish, 0)
     for b in range(rows):
         pltpu.make_async_copy(fc.at[b], corr.at[:, pl.ds(b * bs, bs)], out_sem).start()
-    for p in range(8):
-        mats[p] = fin[p]
+    mats[...] = reduce_basis([fin[p] for p in range(4)], [fin[p] for p in range(4, 8)], step, aug, kvec)
     pltpu.make_async_copy(fc, fc, out_sem).wait()
 
     for j in range(1, LOW):
@@ -471,7 +529,7 @@
         run,
         out_shape=(
             jax.ShapeDtypeStruct(vectors.shape, F32),
-            jax.ShapeDtypeStruct((8, kvec, 128), F32),
+            jax.ShapeDtypeStruct((3 * kvec, 128), F32),
         ),
         in_specs=[smem, smem, hbm, vmem, hbm, hbm, hbm, hbm],
         out_specs=(hbm, vmem),
@@ -497,6 +555,7 @@
             pltpu.VMEM((LOW, kvec, 128), F32),
             pltpu.VMEM((n_high, kvec, 128), F32),
             pltpu.VMEM((8, kvec, 128), F32),
+            pltpu.VMEM((3 * kvec, 256), F32),
             dma((STAGES,)), dma((3,)), dma,
             dma((ITERS + 1,)), dma((ITERS + 1,)), dma((ITERS + 1,)), dma((ITERS + 1,)),
             dma((ITERS, LOW)), dma((ITERS, LOW)), dma((ITERS, n_high)), dma((ITERS, n_high)),
@@ -506,25 +565,7 @@
             collective_id=0, has_side_effects=True, vmem_limit_bytes=60 * 1024 * 1024
         ),
     )(block_cols, live_counts, blocks, onsite_energy.reshape(rows, 1, bs), precond, vectors, prev_vectors, prev_image)
-    gram = mats[0:4].reshape(4 * kvec, 128)
-    proj = mats[4:8].reshape(4 * kvec, 128)
-    step = gram[0:kvec, 96] / (gram[0:kvec, 97] + 1.0)
-
-    def combine(x):
-        x = jnp.concatenate([x[0:64], x[64:96] + step[:, None] * x[96:128]], axis=0)
-        return jnp.concatenate([x[:, 0:64], x[:, 64:96] + step[None, :] * x[:, 96:128]], axis=1)
-
-    lower = combine(gram)
-    tail = lower[64:96]
-    gram_matrix = jnp.concatenate(
-        [jnp.concatenate([lower[0:64, 0:64], tail[:, 0:64].T], axis=1), tail], axis=0
-    )
-    projected = combine(proj)
-    gram_matrix = gram_matrix + jnp.eye(gram_matrix.shape[0], dtype=F32)
-    factor = jnp.linalg.cholesky(gram_matrix)
-    half_way = jax.scipy.linalg.solve_triangular(factor, projected, lower=True)
-    reduced = jax.scipy.linalg.solve_triangular(factor, half_way.T, lower=True).T
-    return correction, reduced
+    return correction, mats[:, 0:3 * kvec]
 
 
 def solution(mesh):

time: 119 us -> 101 us (0.85)
  other arithmetic: 18.6 us -> 0 us
  Pallas kernels: 92.1 us -> 94.8 us
  local copies, waits for them, and re-layouts: 5.95 us -> 4.65 us
    another operation x5 -> x0, other arithmetic: 17.5 us -> none  [the longest x3 9.45 us: local(): factor = jnp.linalg.cholesky(gram_matrix)]
    pallas_call x1, Pallas kernels: 92.1 us -> 94.8 us  [local(): pl.pallas_call(run, out_shape=(jax.ShapeDtypeStruct(vectors.shape, F32),...]
    slice x3 -> x0, local copies, waits for them, and re-layouts: 1.7 us -> none  [the longest x1 0.85 us: local(): gram = mats[0:4].reshape(4 * kvec, 128)]
    unnamed x5 -> x3, local copies, waits for them, and re-layouts: 4.09 us -> 4.65 us
where the time goes in v2:
time: 101 us; the launch traced here: 100 us
  Pallas kernels  94.8 us (94%)
  local copies, waits for them, and re-layouts  4.65 us (5%)
    pallas_call x1, Pallas kernels, local(): pl.pallas_call(run, out_shape=(jax.ShapeDtypeStruct(vectors.shape, F32),...  94.8 us
    unnamed x3, local copies, waits for them, and re-layouts  4.65 us

profile of v2, /device:TPU:0, one launch (start us, length us, event | category | flops | bytes accessed | tf_op | source)
XLA Modules:
  0.0 100.1 jit_solution(14974314643213071847)
XLA Ops:
  0.6 1.4 %copy.10.args_0_ = s32[16,4]{1,0:T(8,128)} copy(s32[16,4]{0,1:T(4,128)} %param.9) | data formatting | bytes 512 | tf_op args[1]
  2.0 94.8 %shard_map.95 = (f32[32,4096]{1,0:T(8,128)}, f32[96,128]{1,0:T(8,128)}) custom-call(s32[16,4]{1,0:T(8,128)} %copy.10.args_0_, s32[16]{0:T(128)} %args_1_.4, f32[16,4,256,256]{3,2,1,0:T(8,128)} %args_2_.4, f32[16,1,256]{2,1,0:T(1,128)} %bitcast.3, f32[16,256,256]{2,1,0:T(8,128)} %args_4_.4, f32[32,4096]{1,0:T(8,128)} %args_5_.4, f32[32,4096]{1,0:T(8,128)} %args_6_.4, ...), custom_call_target="tpu_custom_call" | custom-call | tf_op jit(solution)/shard_map/pallas_call | solution.py:528
  96.8 1.9 %copy.13 = f32[32,4096]{1,0:T(8,128)} copy(f32[32,4096]{1,0:T(8,128)} %get-tuple-element.8) | data formatting | bytes 1048576
  98.7 1.4 %copy.14 = f32[96,96]{1,0:T(8,128)} copy(f32[96,96]{1,0:T(8,128)} %bitcast.2) | data formatting | bytes 73728

commit v3 on v2

--- a/solution.py
+++ b/solution.py
@@ -90,10 +90,10 @@
 def kernel(
     n_dev, rows, kvec, bs,
     cols, live, blocks, onsite, precond, vec, pvec, pimg,
-    corr, mats,
-    stage, bh, bl, ph, plo, offs,
-    fv, fpv, fpi, fim, fr, fu, fhu, fa, fz, fc, fh, zs, acc, qb, sb,
-    zhalo, inc, spill, red1, red2, gram, parts, big1, big2, fin, aug,
+    c_out, u_out, mats,
+    stage, bh, bl, th, tl, ph, plo, offs,
+    fw, fhw, fpv, fpi, fim, fr, fu, fhu, fa, fz, fc, fh, zsw, accw, zs, acc, qb, sb,
+    zhalo, inc, spill, zhalo0, inc0, spill0, red1, red2, gram, parts, big1, big2, fin,
     stage_sem, load_sem, out_sem, zs_sem, zr_sem, ss_sem, sr_sem,
     r1s, r1r, r2s, r2r, b1s, b1r, b2s, b2r, b3s, b3r,
 ):
@@ -106,28 +106,30 @@
     right = lax.rem(me + 1, n_dev)
     left = lax.rem(me + n_dev - 1, n_dev)
     edge = rows - HB
-    order = list(range(edge, rows)) + list(range(edge))
-
-    def load_field(src, dst, sem):
-        for b in range(rows):
-            pltpu.make_async_copy(src.at[:, pl.ds(b * bs, bs)], dst.at[b], sem).start()
-
-    def load_wait(dst, sem):
-        pltpu.make_async_copy(dst, dst, sem).wait()
-
-    n_chunks = rows + rows // SLOTS
-
-    def chunk(i):
-        slot = i % STAGES
-        if i < rows:
-            src = blocks.at[order[i]]
-        else:
-            src = precond.at[pl.ds((i - rows) * SLOTS, SLOTS)]
-        return pltpu.make_async_copy(src, stage.at[slot], stage_sem.at[slot])
-
-    load_field(vec, fv, load_sem.at[0])
-    for i in range(STAGES):
-        chunk(i).start()
+
+    def field_copy(hbm, b):
+        return hbm.at[:, pl.ds(b * bs, bs)]
+
+    def block_copy(row, slot):
+        return pltpu.make_async_copy(blocks.at[row], stage.at[slot], stage_sem.at[slot])
+
+    def precond_copy(j):
+        return pltpu.make_async_copy(precond.at[pl.ds(j * SLOTS, SLOTS)], stage.at[j], stage_sem.at[j])
+
+    def start_loads(b, c):
+        at = pl.ds(pl.multiple_of(b * bs, bs), bs)
+        pltpu.make_async_copy(vec.at[:, at], fw.at[b, pl.ds(0, kvec)], load_sem.at[0]).start()
+        return c
+
+    lax.fori_loop(0, rows, start_loads, 0)
+    for j in range(STAGES):
+        precond_copy(j).start()
+
+    def start_more(b, c):
+        at = pl.ds(pl.multiple_of(b * bs, bs), bs)
+        pltpu.make_async_copy(pvec.at[:, at], fpv.at[b], load_sem.at[1]).start()
+        pltpu.make_async_copy(pimg.at[:, at], fpi.at[b], load_sem.at[2]).start()
+        return c
 
     barrier = pltpu.get_barrier_semaphore()
     peers = [left, right]
@@ -135,7 +137,6 @@
     peers += [lax.rem(high + j, n_high) * LOW + low for j in range(1, n_high)]
     for peer in peers:
         pl.semaphore_signal(barrier, inc=1, device_id=(peer,), device_id_type=MESH)
-    pl.semaphore_wait(barrier, len(peers))
 
     def rcopy(src, dst, s_sem, r_sem, to):
         return pltpu.make_async_remote_copy(
@@ -143,11 +144,13 @@
             device_id=(to,), device_id_type=MESH,
         )
 
-    def z_copy(n, field):
-        return rcopy(field.at[pl.ds(0, HB)], zhalo.at[n], zs_sem.at[n], zr_sem.at[n], left)
+    def z_copy(n):
+        src, dst = (fw, zhalo0) if n == 0 else (fz, zhalo.at[n - 1])
+        return rcopy(src.at[pl.ds(0, HB)], dst, zs_sem.at[n], zr_sem.at[n], left)
 
     def spill_copy(n):
-        return rcopy(spill.at[n], inc.at[n], ss_sem.at[n], sr_sem.at[n], right)
+        src, dst = (spill0, inc0) if n == 0 else (spill.at[n - 1], inc.at[n - 1])
+        return rcopy(src, dst, ss_sem.at[n], sr_sem.at[n], right)
 
     def low_copy(i, j):
         to = high * LOW + lax.rem(low + j, LOW)
@@ -211,195 +214,206 @@
             high_copy(i, j).wait_send()
         return unpack(tile)
 
-    def put_split(b, z):
-        zh, zl = split(z)
-        zs[b, 0:kvec, :] = zh
-        zs[b, kvec:2 * kvec, :] = zl
-
-    def onto(b):
-        zb = zs[b]
-        zh = zb[0:kvec]
-        sums = [None] * (HB + 1)
+    class Apply:
+        def __init__(self, kv, parts_ref, acc_ref):
+            self.kv, self.zs, self.acc = kv, parts_ref, acc_ref
+
+        def put(self, b, z):
+            zh, zl = split(z)
+            self.zs[b, 0:self.kv, :] = zh
+            self.zs[b, self.kv:2 * self.kv, :] = zl
+
+        def diag(self, b, z):
+            self.acc[b] = onsite[b] * z
+
+        def clear_tail(self):
+            for t in range(HB):
+                self.acc[rows + t] = jnp.zeros((self.kv, bs), F32)
+
+        def product(self, z, hi, lo):
+            part = mm(z, hi)
+            return part[0:self.kv] + part[self.kv:] + mm(z[0:self.kv], lo)
+
+        def onto(self, b):
+            zb = self.zs[b]
+            sums = [None] * (HB + 1)
+            for s in range(SLOTS):
+                moved = self.product(zb, bh[b * SLOTS + s], bl[b * SLOTS + s])
+                off = offs[b * SLOTS + s]
+                for o in range(HB + 1):
+                    term = jnp.where(off == o, 1.0, 0.0) * moved
+                    sums[o] = term if sums[o] is None else sums[o] + term
+            for o in range(HB + 1):
+                self.acc[b + o] = self.acc[b + o] + sums[o]
+
+        def across(self, b):
+            out = None
+            for s in range(SLOTS):
+                term = self.product(self.zs[b + offs[b * SLOTS + s]], th[b * SLOTS + s], tl[b * SLOTS + s])
+                out = term if out is None else out + term
+            self.acc[b] = self.acc[b] + out
+
+        def halo_in(self, n):
+            z_copy(n).wait_recv()
+            for t in range(HB):
+                self.put(rows + t, zhalo0[t] if n == 0 else zhalo[n - 1, t])
+
+        def send_spill(self, n):
+            for t in range(HB):
+                if n == 0:
+                    spill0[t] = self.acc[rows + t]
+                else:
+                    spill[n - 1, t] = self.acc[rows + t]
+            spill_copy(n).start()
+
+        def take_in(self, n):
+            spill_copy(n).wait_recv()
+            for t in range(HB):
+                self.acc[t] = self.acc[t] + (inc0[t] if n == 0 else inc[n - 1, t])
+
+    wide = Apply(2 * kvec, zsw, accw)
+    thin = Apply(kvec, zs, acc)
+
+    def precondition(x, b):
+        dh, dl = split(x)
+        part = mm(jnp.concatenate([dh, dl], axis=0), ph[b])
+        return part[0:kvec] + part[kvec:] + mm(dh, plo[b])
+
+    pltpu.make_async_copy(fw.at[:, pl.ds(0, kvec)], fw.at[:, pl.ds(0, kvec)], load_sem.at[0]).wait()
+    for j in range(rows // SLOTS):
+        precond_copy(j).wait()
+        for t in range(SLOTS):
+            b = j * SLOTS + t
+            xh, xl = split(stage[j, t])
+            ph[b] = xh.T
+            plo[b] = xl.T
+        block_copy(edge + j, j).start()
+        for t in range(SLOTS):
+            b = j * SLOTS + t
+            v = fw[b, 0:kvec]
+            fw[b, kvec:2 * kvec] = precondition(v, b)
+            x = fw[b]
+            wide.put(b, x)
+            wide.diag(b, x)
+        if j == 0:
+            pl.semaphore_wait(barrier, len(peers))
+            z_copy(0).start()
+    lax.fori_loop(0, rows, start_more, 0)
+    wide.clear_tail()
+
+    def take_row(b, slot):
+        block_copy(b, slot).wait()
         for s in range(SLOTS):
-            part = mm(zb, bh[b * SLOTS + s])
-            moved = part[0:kvec] + part[kvec:] + mm(zh, bl[b * SLOTS + s])
-            off = offs[b * SLOTS + s]
-            for o in range(HB + 1):
-                term = jnp.where(off == o, 1.0, 0.0) * moved
-                sums[o] = term if sums[o] is None else sums[o] + term
-        for o in range(HB + 1):
-            acc[b + o] = acc[b + o] + sums[o]
-
-    def across(b):
-        out = None
-        for s in range(SLOTS):
-            zc = zs[b + offs[b * SLOTS + s]]
-            part = mmt(zc, bh[b * SLOTS + s])
-            term = part[0:kvec] + part[kvec:] + mmt(zc[0:kvec], bl[b * SLOTS + s])
-            out = term if out is None else out + term
-        acc[b] = acc[b] + out
-
-    def halo_in(n):
-        z_copy(n, fv).wait_recv()
-        for t in range(HB):
-            put_split(rows + t, zhalo[n, t])
-
-    def send_spill(n):
-        for t in range(HB):
-            spill[n, t] = acc[rows + t]
-        spill_copy(n).start()
-
-    def take_in(n):
-        spill_copy(n).wait_recv()
-        for t in range(HB):
-            acc[t] = acc[t] + inc[n, t]
-
-    def diag(b, z):
-        acc[b] = onsite[b] * z
-
-    def clear_tail():
-        for t in range(HB):
-            acc[rows + t] = jnp.zeros((kvec, bs), F32)
-
-    load_wait(fv, load_sem.at[0])
-    z_copy(0, fv).start()
-    load_field(pvec, fpv, load_sem.at[1])
-    load_field(pimg, fpi, load_sem.at[2])
-
-    def prepare(b, c):
-        z = fv[b]
-        put_split(b, z)
-        diag(b, z)
+            off = cols[s, b] - first - b
+            off = jnp.where(off < 0, off + total, off)
+            offs[b * SLOTS + s] = jnp.minimum(off, HB)
+            alive = jnp.where(s < live[b], 1.0, 0.0)
+            xh, xl = split(stage[slot, s] * alive)
+            bh[b * SLOTS + s] = xh
+            bl[b * SLOTS + s] = xl
+            th[b * SLOTS + s] = xh.T
+            tl[b * SLOTS + s] = xl.T
+
+    def tail_row(i, c):
+        take_row(edge + i, i)
+        block_copy(i, i).start()
+        wide.onto(edge + i)
         return c
 
-    lax.fori_loop(0, rows, prepare, 0)
-    clear_tail()
-
-    def take_chunk(i):
-        chunk(i).wait()
-        slot = i % STAGES
-        if i < rows:
-            b = order[i]
-            for s in range(SLOTS):
-                off = lax.rem(cols[b, s] - first - b + 2 * total, total)
-                offs[b * SLOTS + s] = jnp.minimum(off, HB)
-                alive = jnp.where(s < live[b], 1.0, 0.0)
-
-                def piece(p, c):
-                    at = pl.ds(pl.multiple_of(p * 64, 64), 64)
-                    xh, xl = split(stage[slot, s, at, :] * alive)
-                    bh[b * SLOTS + s, at, :] = xh
-                    bl[b * SLOTS + s, at, :] = xl
-                    return c
-
-                lax.fori_loop(0, bs // 64, piece, 0)
-        else:
-            for s in range(SLOTS):
-                def piece(p, c):
-                    at = pl.ds(pl.multiple_of(p * 64, 64), 64)
-                    xh, xl = split(stage[slot, s, at, :])
-                    ph[(i - rows) * SLOTS + s, at, :] = xh
-                    plo[(i - rows) * SLOTS + s, at, :] = xl
-                    return c
-
-                lax.fori_loop(0, bs // 64, piece, 0)
-        if i + STAGES < n_chunks:
-            chunk(i + STAGES).start()
-
-    for i in range(HB):
-        take_chunk(i)
-        onto(order[i])
-    send_spill(0)
-    for i in range(HB, rows):
-        take_chunk(i)
-        onto(order[i])
-        across(order[i])
-    halo_in(0)
+    lax.fori_loop(0, HB, tail_row, 0)
+    wide.send_spill(0)
+
+    def head_row(b, c):
+        slot = lax.rem(b, STAGES)
+        take_row(b, slot)
+
+        @pl.when(b + STAGES < edge)
+        def _():
+            block_copy(b + STAGES, slot).start()
+
+        wide.onto(b)
+        wide.across(b)
+        return c
+
+    lax.fori_loop(0, edge, head_row, 0)
+    wide.halo_in(0)
     for b in range(edge, rows):
-        across(b)
-    take_in(0)
+        wide.across(b)
+    wide.take_in(0)
 
     zero = jnp.zeros((kvec, bs), F32)
 
     def first_sums(b, c):
-        x, im = fv[b], acc[b]
+        x = fw[b, 0:kvec]
+        im = accw[b, 0:kvec]
         fim[b] = im
+        fhw[b] = accw[b, kvec:2 * kvec]
         return c[0] + x * im, c[1] + x * x
 
     num, den = lax.fori_loop(0, rows, first_sums, (zero, zero))
     total_of = lambda x: jnp.sum(x, axis=1, keepdims=True)
     red_start(0, total_of(num), total_of(den))
-    for i in range(rows, n_chunks):
-        take_chunk(i)
-    red_mid(0)
-    num, den = red_end(0)
-    q = num / den
-    qb[...] = jnp.broadcast_to(q, (kvec, bs))
-
-    def first_rest(b, c):
-        fr[b] = qb[...] * fv[b] - fim[b]
-        return c
-
-    lax.fori_loop(0, rows, first_rest, 0)
-
-    def precondition(field, b):
-        dh, dl = split(field[b])
-        both = jnp.concatenate([dh, dl], axis=0)
-        part = mmt(both, ph[b])
-        z = part[0:kvec] + part[kvec:] + mmt(dh, plo[b])
-        fz[b] = z
-        put_split(b, z)
-        diag(b, z)
 
     for k in range(ITERS):
         n = k + 1
-        field = fr if k == 0 else fa
+        field = fim if k == 0 else fa
+
+        def prepare(b, field=field):
+            z = precondition(field[b], b)
+            fz[b] = z
+            thin.put(b, z)
+            thin.diag(b, z)
+
         for b in range(HB):
-            precondition(field, b)
-        z_copy(n, fz).start()
-        clear_tail()
+            prepare(b)
+        z_copy(n).start()
+        thin.clear_tail()
         for b in range(edge, rows):
-            precondition(field, b)
+            prepare(b)
         for b in range(edge, rows):
-            onto(b)
-        send_spill(n)
-
-        def interior(g, c, field=field):
+            thin.onto(b)
+        thin.send_spill(n)
+
+        def interior(g, c, prepare=prepare):
             for t in range(4):
-                precondition(field, 4 + 4 * g + t)
+                prepare(4 + 4 * g + t)
             return c
 
         lax.fori_loop(0, (edge - HB) // 4, interior, 0)
-        if k > 0:
-            red_mid(k)
+        red_mid(k)
 
         def body(g, c):
             for t in range(4):
-                onto(4 * g + t)
+                thin.onto(4 * g + t)
             for t in range(4):
-                across(4 * g + t)
+                thin.across(4 * g + t)
             return c
 
         lax.fori_loop(0, edge // 4, body, 0)
-        halo_in(n)
+        thin.halo_in(n)
         for b in range(edge, rows):
-            across(b)
-        take_in(n)
-        z_copy(n, fz).wait_send()
-        if k > 0:
-            cross, own = red_end(k)
-            step = cross / (own + 1.0)
-            sb[...] = jnp.broadcast_to(step, (kvec, bs))
+            thin.across(b)
+        thin.take_in(n)
+        z_copy(n).wait_send()
+        top, bottom = red_end(k)
+        if k == 0:
+            qb[...] = jnp.broadcast_to(top / bottom, (kvec, bs))
+        else:
+            sb[...] = jnp.broadcast_to(top / (bottom + 1.0), (kvec, bs))
 
         def update(b, c, k=k):
             z, hz = fz[b], acc[b]
-            m = hz - qb[...] * z
+            q = qb[...]
             if k == 0:
-                r = fr[b]
-                a = m
-                fu[b] = z
-                fhu[b] = hz
+                u = q * fw[b, kvec:2 * kvec] - z
+                hu = q * fhw[b] - hz
+                r = q * fw[b, 0:kvec] - fim[b]
+                a = hu - q * u
+                fu[b] = u
+                fhu[b] = hu
+                fr[b] = r
             else:
+                m = hz - q * z
                 s = sb[...]
                 u, hu, a = fu[b], fhu[b], fa[b]
                 r = fr[b] - s * a
@@ -420,12 +434,18 @@
         if k + 1 < ITERS:
             red_start(k + 1, total_of(cross), total_of(own))
 
-    load_wait(fpv, load_sem.at[1])
-    load_wait(fpi, load_sem.at[2])
+    def put_out(b, c):
+        at = pl.ds(pl.multiple_of(b * bs, bs), bs)
+        pltpu.make_async_copy(fc.at[b], c_out.at[:, at], out_sem.at[0]).start()
+        pltpu.make_async_copy(fu.at[b], u_out.at[:, at], out_sem.at[1]).start()
+        return c
+
+    pltpu.make_async_copy(fpv, fpv, load_sem.at[1]).wait()
+    pltpu.make_async_copy(fpi, fpi, load_sem.at[2]).wait()
     gram[...] = jnp.zeros_like(gram)
 
     def products(b, c):
-        xh, xl = split(jnp.concatenate([fv[b], fpv[b], fc[b], fu[b]], axis=0))
+        xh, xl = split(jnp.concatenate([fw[b, 0:kvec], fpv[b], fc[b], fu[b]], axis=0))
         yh, yl = split(jnp.concatenate([fim[b], fpi[b], fh[b], fhu[b]], axis=0))
         part = mmt(jnp.concatenate([xh, xl], axis=0), jnp.concatenate([xh, yh], axis=0))
         m = xh.shape[0]
@@ -433,12 +453,12 @@
         return c
 
     lax.fori_loop(0, rows, products, 0)
-    wide = lax.broadcasted_iota(jnp.int32, (kvec, 128), 1)
+    span = lax.broadcasted_iota(jnp.int32, (kvec, 128), 1)
     for p in range(4):
         at = pl.ds(p * kvec, kvec)
         g = gram[at, 0:128]
         if p == 0:
-            g = jnp.where(wide == 96, total_of(cross), jnp.where(wide == 97, total_of(own), g))
+            g = jnp.where(span == 96, total_of(cross), jnp.where(span == 97, total_of(own), g))
         parts[p] = g
         parts[4 + p] = gram[at, 128:256]
 
@@ -468,6 +488,7 @@
 
     for j in range(1, LOW):
         big1_copy(j).start()
+    lax.fori_loop(0, rows, put_out, 0)
     big1[low] = parts[low]
     for j in range(1, LOW):
         big1_in(j).wait_recv()
@@ -488,28 +509,43 @@
     for j in range(1, LOW):
         fin_in(j).wait_recv()
 
-    head = fin[0]
-    step = head[:, 96:97] / (head[:, 97:98] + 1.0)
-    sb[...] = jnp.broadcast_to(step, (kvec, bs))
-
-    def finish(b, c):
-        fc[b] = fc[b] + sb[...] * fu[b]
-        return c
-
-    lax.fori_loop(0, rows, finish, 0)
-    for b in range(rows):
-        pltpu.make_async_copy(fc.at[b], corr.at[:, pl.ds(b * bs, bs)], out_sem).start()
-    mats[...] = reduce_basis([fin[p] for p in range(4)], [fin[p] for p in range(4, 8)], step, aug, kvec)
-    pltpu.make_async_copy(fc, fc, out_sem).wait()
+    for p in range(8):
+        mats[p] = fin[p]
+    pltpu.make_async_copy(fc, fc, out_sem.at[0]).wait()
+    pltpu.make_async_copy(fu, fu, out_sem.at[1]).wait()
 
     for j in range(1, LOW):
         big1_copy(j).wait_send()
         fin_copy(j).wait_send()
     for j in range(1, n_high):
         big2_copy(j).wait_send()
-    z_copy(0, fv).wait_send()
+    z_copy(0).wait_send()
     for n in range(ITERS + 1):
         spill_copy(n).wait_send()
+
+
+def finish(kvec, c_in, u_in, fin, corr, reduced, cbuf, ubuf, aug, sem):
+    first = pltpu.make_async_copy(c_in, cbuf, sem.at[0])
+    second = pltpu.make_async_copy(u_in, ubuf, sem.at[1])
+    first.start()
+    second.start()
+    head = fin[0]
+    step = head[:, 96:97] / (head[:, 97:98] + 1.0)
+    wide = jnp.broadcast_to(step, (kvec, 512))
+    first.wait()
+    second.wait()
+
+    def add(g, c):
+        at = pl.ds(pl.multiple_of(g * 512, 512), 512)
+        cbuf[:, at] = cbuf[:, at] + wide * ubuf[:, at]
+        return c
+
+    lax.fori_loop(0, cbuf.shape[1] // 512, add, 0)
+    third = pltpu.make_async_copy(cbuf, corr, sem.at[2])
+    third.start()
+    full = reduce_basis([fin[p] for p in range(4)], [fin[p] for p in range(4, 8)], step, aug, kvec)
+    reduced[...] = full[:, 0:3 * kvec]
+    third.wait()
 
 
 def local(n_dev, blocks, block_cols, live_counts, onsite_energy, precond, vectors, prev_vectors, prev_image):
@@ -517,6 +553,7 @@
     kvec = vectors.shape[0]
     n_high = n_dev // LOW
     field = pltpu.VMEM((rows, kvec, bs), F32)
+    tiles = pltpu.VMEM((rows * slots, bs, bs), BF16)
     dma = pltpu.SemaphoreType.DMA
     hbm = pl.BlockSpec(memory_space=pl.ANY)
     smem = pl.BlockSpec(memory_space=pltpu.SMEM)
@@ -525,29 +562,35 @@
     def run(*args):
         return kernel(n_dev, rows, kvec, bs, *args)
 
-    correction, mats = pl.pallas_call(
+    mid, last, mats = pl.pallas_call(
         run,
         out_shape=(
             jax.ShapeDtypeStruct(vectors.shape, F32),
-            jax.ShapeDtypeStruct((3 * kvec, 128), F32),
+            jax.ShapeDtypeStruct(vectors.shape, F32),
+            jax.ShapeDtypeStruct((8, kvec, 128), F32),
         ),
         in_specs=[smem, smem, hbm, vmem, hbm, hbm, hbm, hbm],
-        out_specs=(hbm, vmem),
+        out_specs=(hbm, hbm, vmem),
         scratch_shapes=[
             pltpu.VMEM((STAGES, slots, bs, bs), F32),
-            pltpu.VMEM((rows * slots, bs, bs), BF16),
-            pltpu.VMEM((rows * slots, bs, bs), BF16),
+            tiles, tiles, tiles, tiles,
             pltpu.VMEM((rows, bs, bs), BF16),
             pltpu.VMEM((rows, bs, bs), BF16),
             pltpu.SMEM((rows * slots,), jnp.int32),
+            pltpu.VMEM((rows, 2 * kvec, bs), F32),
             field, field, field, field, field, field, field, field, field, field, field,
+            pltpu.VMEM((rows + HB, 4 * kvec, bs), BF16),
+            pltpu.VMEM((rows + HB, 2 * kvec, bs), F32),
             pltpu.VMEM((rows + HB, 2 * kvec, bs), BF16),
             pltpu.VMEM((rows + HB, kvec, bs), F32),
             pltpu.VMEM((kvec, bs), F32),
             pltpu.VMEM((kvec, bs), F32),
-            pltpu.VMEM((ITERS + 1, HB, kvec, bs), F32),
-            pltpu.VMEM((ITERS + 1, HB, kvec, bs), F32),
-            pltpu.VMEM((ITERS + 1, HB, kvec, bs), F32),
+            pltpu.VMEM((ITERS, HB, kvec, bs), F32),
+            pltpu.VMEM((ITERS, HB, kvec, bs), F32),
+            pltpu.VMEM((ITERS, HB, kvec, bs), F32),
+            pltpu.VMEM((HB, 2 * kvec, bs), F32),
+            pltpu.VMEM((HB, 2 * kvec, bs), F32),
+            pltpu.VMEM((HB, 2 * kvec, bs), F32),
             pltpu.VMEM((ITERS, LOW, 8, 128), F32),
             pltpu.VMEM((ITERS, n_high, 8, 128), F32),
             pltpu.VMEM((4 * kvec, 256), F32),
@@ -555,17 +598,34 @@
             pltpu.VMEM((LOW, kvec, 128), F32),
             pltpu.VMEM((n_high, kvec, 128), F32),
             pltpu.VMEM((8, kvec, 128), F32),
-            pltpu.VMEM((3 * kvec, 256), F32),
-            dma((STAGES,)), dma((3,)), dma,
+            dma((STAGES,)), dma((3,)), dma((2,)),
             dma((ITERS + 1,)), dma((ITERS + 1,)), dma((ITERS + 1,)), dma((ITERS + 1,)),
             dma((ITERS, LOW)), dma((ITERS, LOW)), dma((ITERS, n_high)), dma((ITERS, n_high)),
             dma((LOW,)), dma((LOW,)), dma((n_high,)), dma((n_high,)), dma((LOW,)), dma((LOW,)),
         ],
         compiler_params=pltpu.CompilerParams(
-            collective_id=0, has_side_effects=True, vmem_limit_bytes=60 * 1024 * 1024
+            collective_id=0, has_side_effects=True, vmem_limit_bytes=63 * 1024 * 1024
         ),
-    )(block_cols, live_counts, blocks, onsite_energy.reshape(rows, 1, bs), precond, vectors, prev_vectors, prev_image)
-    return correction, mats[:, 0:3 * kvec]
+    )(block_cols.T, live_counts, blocks, onsite_energy.reshape(rows, 1, bs), precond, vectors, prev_vectors, prev_image)
+
+    def run_last(*args):
+        return finish(kvec, *args)
+
+    return pl.pallas_call(
+        run_last,
+        out_shape=(
+            jax.ShapeDtypeStruct(vectors.shape, F32),
+            jax.ShapeDtypeStruct((3 * kvec, 3 * kvec), F32),
+        ),
+        in_specs=[hbm, hbm, vmem],
+        out_specs=(hbm, vmem),
+        scratch_shapes=[
+            pltpu.VMEM(vectors.shape, F32),
+            pltpu.VMEM(vectors.shape, F32),
+            pltpu.VMEM((3 * kvec, 256), F32),
+            dma((3,)),
+        ],
+    )(mid, last, mats)
 
 
 def solution(mesh):

time: 101 us -> 77.3 us (0.77)
  Pallas kernels: 94.8 us -> 75.3 us
  local copies, waits for them, and re-layouts: 4.65 us -> 0 us
    pallas_call x1, Pallas kernels: 94.8 us -> 69.2 us  [local(): pl.pallas_call(run, out_shape=(jax.ShapeDtypeStruct(vectors.shape, F32),...]
    pallas_call x0 -> x1, Pallas kernels: none -> 6.13 us  [local(): pl.pallas_call(run_last, out_shape=(jax.ShapeDtypeStruct(vectors.shape, F...]
    unnamed x3 -> x0, local copies, waits for them, and re-layouts: 4.65 us -> none
where the time goes in v3:
time: 77.3 us; the launch traced here: 76.1 us
  Pallas kernels  75.3 us (97%)
  between operations  0.8 us (1%)
    pallas_call x1, Pallas kernels, local(): pl.pallas_call(run, out_shape=(jax.ShapeDtypeStruct(vectors.shape, F32),...  69.2 us
    pallas_call x1, Pallas kernels, local(): pl.pallas_call(run_last, out_shape=(jax.ShapeDtypeStruct(vectors.shape, F...  6.13 us

profile of v3, /device:TPU:0, one launch (start us, length us, event | category | flops | bytes accessed | tf_op | source)
XLA Modules:
  0.0 76.1 jit_solution(33099612910587639)
XLA Ops:
  0.6 69.2 %shard_map.95 = (f32[32,4096]{1,0:T(8,128)}, f32[32,4096]{1,0:T(8,128)}, f32[8,32,128]{2,1,0:T(8,128)}) custom-call(s32[4,16]{1,0:T(4,128)} %bitcast.3, s32[16]{0:T(128)} %args_1_.4, f32[16,4,256,256]{3,2,1,0:T(8,128)} %args_2_.4, f32[16,1,256]{2,1,0:T(1,128)} %bitcast.2, f32[16,256,256]{2,1,0:T(8,128)} %args_4_.4, f32[32,4096]{1,0:T(8,128)} %args_5_.4, ...), custom_call_target="tpu_custom_call" | custom-call | tf_op jit(solution)/shard_map/pallas_call | solution.py:565
  69.8 6.1 %shard_map.96 = (f32[32,4096]{1,0:T(8,128)}, f32[96,96]{1,0:T(8,128)}) custom-call(f32[32,4096]{1,0:T(8,128)} %get-tuple-element.5.args_0_, f32[32,4096]{1,0:T(8,128)} %get-tuple-element.6.args_1_, f32[8,32,128]{2,1,0:T(8,128)} %get-tuple-element.7.args_2_), custom_call_target="tpu_custom_call" | custom-call | tf_op jit(solution)/shard_map/pallas_call | solution.py:614

commit v4 on v3

--- a/solution.py
+++ b/solution.py
@@ -28,31 +28,45 @@
     return lax.dot_general(a, b, (((1,), (1,)), ((), ())), preferred_element_type=F32)
 
 
-def reduce_basis(gram, proj, step, aug, kvec):
+def reduce_basis(early, late, step, aug, kvec, between):
     width = 128
     size = 3 * kvec
     lane = lax.broadcasted_iota(jnp.int32, (kvec, width), 1)
     row = lax.broadcasted_iota(jnp.int32, (kvec, width), 0)
-    step_row = jnp.sum(jnp.where(lane == row + size, step, 0.0), axis=0, keepdims=True)
-
-    def fold(x):
-        n = x.shape[0]
-        at = lax.broadcasted_iota(jnp.int32, (n, width), 1)
-        moved = pltpu.roll(x * step_row, width - kvec, 1)
-        return jnp.where(at < 2 * kvec, x, jnp.where(at < size, x + moved, 0.0))
-
-    tail = fold(gram[2] + step * gram[3])
-    above = jnp.concatenate([jnp.zeros((2 * kvec, width), F32), tail, jnp.zeros((kvec, width), F32)], axis=0).T
+    step_col = jnp.sum(jnp.where(lane == row + 2 * kvec, step, 0.0), axis=0, keepdims=True)
+    rest = jnp.zeros((2 * kvec, width), F32)
+
+    def turned(x):
+        return jnp.concatenate([rest, x, jnp.zeros((kvec, width), F32)], axis=0).T
+
+    lead = lane < 2 * kvec
+    side = (lane >= 2 * kvec) & (lane < size)
+    g_c, g_u, p_c, p_u = late
+    mixed = g_c + step * g_u
+    flip = turned(jnp.where(lead, mixed, g_u))
+    square = mixed + step_col * (flip[2 * kvec:size] + step * pltpu.roll(g_u, width - kvec, 1))
+    tail = jnp.where(side, square, jnp.where(lead, mixed, 0.0))
     for g in range(2):
-        a = jnp.where(lane < 2 * kvec, gram[g], above[g * kvec:(g + 1) * kvec])
+        a = jnp.where(lead, early[g], jnp.where(side, flip[g * kvec:(g + 1) * kvec], 0.0))
         aug[g * kvec:(g + 1) * kvec, 0:width] = a + jnp.where(lane == row + g * kvec, 1.0, 0.0)
     aug[2 * kvec:size, 0:width] = tail + jnp.where(lane == row + 2 * kvec, 1.0, 0.0)
     for g in range(3):
         aug[g * kvec:(g + 1) * kvec, width:2 * width] = jnp.where(lane == row + g * kvec, 1.0, 0.0)
-    x = jnp.concatenate([fold(proj[0]), fold(proj[1]), fold(proj[2] + step * proj[3]), jnp.zeros((kvec, width), F32)], axis=0)
+    mixed = p_c + step * p_u
+    cross = pltpu.roll(g_c + step * p_c, 2 * kvec, 1)
+    flip = turned(jnp.where(lane < kvec, mixed, jnp.where(lead, cross, p_u)))
+    square = mixed + step_col * (flip[2 * kvec:size] + step * pltpu.roll(p_u, width - kvec, 1))
+    x = []
+    for g in range(2):
+        moved = pltpu.roll(early[g], 2 * kvec, 1)
+        x.append(jnp.where(lead, moved, jnp.where(side, flip[g * kvec:(g + 1) * kvec], 0.0)))
+    x.append(jnp.where(side, square, jnp.where(lead, mixed, 0.0)))
+    x = jnp.concatenate(x + [jnp.zeros((kvec, width), F32)], axis=0)
 
     sub = lax.broadcasted_iota(jnp.int32, (8, width), 0)
     for top in range(0, size, 8):
+        if top == 2 * kvec:
+            between()
         n = size - top
         cols = [jnp.broadcast_to(aug[top:size, top + c:top + c + 1], (n, width)) for c in range(8)]
         pivot_rows = aug[top:top + 8, :]
@@ -90,12 +104,12 @@
 def kernel(
     n_dev, rows, kvec, bs,
     cols, live, blocks, onsite, precond, vec, pvec, pimg,
-    c_out, u_out, mats,
+    c_out, u_out, early_out, late_out, sums_out,
     stage, bh, bl, th, tl, ph, plo, offs,
     fw, fhw, fpv, fpi, fim, fr, fu, fhu, fa, fz, fc, fh, zsw, accw, zs, acc, qb, sb,
-    zhalo, inc, spill, zhalo0, inc0, spill0, red1, red2, gram, parts, big1, big2, fin,
+    zhalo, inc, spill, zhalo0, inc0, spill0, red1, red2, gram, early, early1, early2, early3, parts, big1, big2, fin,
     stage_sem, load_sem, out_sem, zs_sem, zr_sem, ss_sem, sr_sem,
-    r1s, r1r, r2s, r2r, b1s, b1r, b2s, b2r, b3s, b3r,
+    r1s, r1r, r2s, r2r, b1s, b1r, b2s, b2r, b3s, b3r, e1s, e1r, e2s, e2r, e3s, e3r,
 ):
     me = lax.axis_index("rows")
     low = lax.rem(me, LOW)
@@ -213,6 +227,73 @@
         for j in range(1, n_high):
             high_copy(i, j).wait_send()
         return unpack(tile)
+
+    class Exchange:
+        def __init__(self, src, near, far, out, sems):
+            self.src, self.near, self.far, self.out, self.sems = src, near, far, out, sems
+
+        def near_copy(self, j):
+            to = lax.rem(low + j, LOW)
+            return rcopy(self.src.at[to], self.near.at[low], self.sems[0].at[j], self.sems[1].at[low], high * LOW + to)
+
+        def near_in(self, j):
+            frm = lax.rem(low + j, LOW)
+            return rcopy(self.src.at[frm], self.near.at[frm], self.sems[0].at[j], self.sems[1].at[frm], left)
+
+        def far_copy(self, j):
+            to = lax.rem(high + j, n_high) * LOW + low
+            return rcopy(self.far.at[high], self.far.at[high], self.sems[2].at[j], self.sems[3].at[high], to)
+
+        def far_in(self, j):
+            frm = lax.rem(high + j, n_high)
+            return rcopy(self.far.at[frm], self.far.at[frm], self.sems[2].at[j], self.sems[3].at[frm], left)
+
+        def back_copy(self, j):
+            to = high * LOW + lax.rem(low + j, LOW)
+            return rcopy(self.out.at[low], self.out.at[low], self.sems[4].at[j], self.sems[5].at[low], to)
+
+        def back_in(self, j):
+            frm = lax.rem(low + j, LOW)
+            return rcopy(self.out.at[frm], self.out.at[frm], self.sems[4].at[j], self.sems[5].at[frm], left)
+
+        def start(self):
+            for j in range(1, LOW):
+                self.near_copy(j).start()
+            self.near[low] = self.src[low]
+
+        def middle(self):
+            for j in range(1, LOW):
+                self.near_in(j).wait_recv()
+            tile = self.near[0]
+            for l in range(1, LOW):
+                tile = tile + self.near[l]
+            self.far[high] = tile
+            for j in range(1, n_high):
+                self.far_copy(j).start()
+
+        def back(self):
+            for j in range(1, n_high):
+                self.far_in(j).wait_recv()
+            tile = self.far[0]
+            for l in range(1, n_high):
+                tile = tile + self.far[l]
+            self.out[low] = tile
+            for j in range(1, LOW):
+                self.back_copy(j).start()
+
+        def end(self):
+            for j in range(1, LOW):
+                self.back_in(j).wait_recv()
+
+        def drain(self):
+            for j in range(1, LOW):
+                self.near_copy(j).wait_send()
+                self.back_copy(j).wait_send()
+            for j in range(1, n_high):
+                self.far_copy(j).wait_send()
+
+    soon = Exchange(early, early1, early2, early3, (e1s, e1r, e2s, e2r, e3s, e3r))
+    later = Exchange(parts, big1, big2, fin, (b1s, b1r, b2s, b2r, b3s, b3r))
 
     class Apply:
         def __init__(self, kv, parts_ref, acc_ref):
@@ -354,6 +435,20 @@
     total_of = lambda x: jnp.sum(x, axis=1, keepdims=True)
     red_start(0, total_of(num), total_of(den))
 
+    pltpu.make_async_copy(fpv, fpv, load_sem.at[1]).wait()
+    pltpu.make_async_copy(fpi, fpi, load_sem.at[2]).wait()
+
+    def old_products(b, c):
+        xh, xl = split(jnp.concatenate([fw[b, 0:kvec], fpv[b], fim[b], fpi[b]], axis=0))
+        m = 2 * kvec
+        part = mmt(jnp.concatenate([xh[0:m], xl[0:m]], axis=0), xh)
+        return c + (part[0:m] + part[m:] + mmt(xh[0:m], xl))
+
+    old = lax.fori_loop(0, rows, old_products, jnp.zeros((2 * kvec, 128), F32))
+    for p in range(8):
+        early[p] = old[8 * p:8 * p + 8]
+    soon.start()
+
     for k in range(ITERS):
         n = k + 1
         field = fim if k == 0 else fa
@@ -379,8 +474,10 @@
                 prepare(4 + 4 * g + t)
             return c
 
-        lax.fori_loop(0, (edge - HB) // 4, interior, 0)
+        for g in range((edge - HB) // 4):
+            interior(g, 0)
         red_mid(k)
+        (soon.middle, soon.back, soon.end)[k]()
 
         def body(g, c):
             for t in range(4):
@@ -389,7 +486,8 @@
                 thin.across(4 * g + t)
             return c
 
-        lax.fori_loop(0, edge // 4, body, 0)
+        for g in range(edge // 4):
+            body(g, 0)
         thin.halo_in(n)
         for b in range(edge, rows):
             thin.across(b)
@@ -440,110 +538,80 @@
         pltpu.make_async_copy(fu.at[b], u_out.at[:, at], out_sem.at[1]).start()
         return c
 
-    pltpu.make_async_copy(fpv, fpv, load_sem.at[1]).wait()
-    pltpu.make_async_copy(fpi, fpi, load_sem.at[2]).wait()
+    red_start(ITERS, total_of(cross), total_of(own))
+    lax.fori_loop(0, rows, put_out, 0)
+
     gram[...] = jnp.zeros_like(gram)
 
     def products(b, c):
         xh, xl = split(jnp.concatenate([fw[b, 0:kvec], fpv[b], fc[b], fu[b]], axis=0))
         yh, yl = split(jnp.concatenate([fim[b], fpi[b], fh[b], fhu[b]], axis=0))
-        part = mmt(jnp.concatenate([xh, xl], axis=0), jnp.concatenate([xh, yh], axis=0))
-        m = xh.shape[0]
-        gram[...] = gram[...] + (part[0:m] + part[m:] + mmt(xh, jnp.concatenate([xl, yl], axis=0)))
+        m = 2 * kvec
+        left_side = jnp.concatenate([xh[m:], yh[m:], xl[m:], yl[m:]], axis=0)
+        part = mmt(left_side, jnp.concatenate([xh, yh], axis=0))
+        n = 2 * m
+        gram[...] = gram[...] + (part[0:n] + part[n:] + mmt(left_side[0:n], jnp.concatenate([xl, yl], axis=0)))
         return c
 
     lax.fori_loop(0, rows, products, 0)
+    red_mid(ITERS)
     span = lax.broadcasted_iota(jnp.int32, (kvec, 128), 1)
+    hp = pltpu.roll(gram[2 * kvec:3 * kvec, 0:128], 64, 1)
+    hup = pltpu.roll(gram[3 * kvec:4 * kvec, 0:128], 64, 1)
+    last = span >= 3 * kvec
+    quarters = (
+        jnp.where(last, hp, gram[0:kvec, 0:128]),
+        gram[kvec:2 * kvec, 0:128],
+        jnp.where(last, hup, gram[0:kvec, 128:256]),
+        gram[kvec:2 * kvec, 128:256],
+    )
     for p in range(4):
-        at = pl.ds(p * kvec, kvec)
-        g = gram[at, 0:128]
-        if p == 0:
-            g = jnp.where(span == 96, total_of(cross), jnp.where(span == 97, total_of(own), g))
-        parts[p] = g
-        parts[4 + p] = gram[at, 128:256]
-
-    def big1_copy(j):
-        to = lax.rem(low + j, LOW)
-        return rcopy(parts.at[to], big1.at[low], b1s.at[j], b1r.at[low], high * LOW + to)
-
-    def big1_in(j):
-        frm = lax.rem(low + j, LOW)
-        return rcopy(parts.at[frm], big1.at[frm], b1s.at[j], b1r.at[frm], left)
-
-    def big2_copy(j):
-        to = lax.rem(high + j, n_high) * LOW + low
-        return rcopy(big2.at[high], big2.at[high], b2s.at[j], b2r.at[high], to)
-
-    def big2_in(j):
-        frm = lax.rem(high + j, n_high)
-        return rcopy(big2.at[frm], big2.at[frm], b2s.at[j], b2r.at[frm], left)
-
-    def fin_copy(j):
-        to = high * LOW + lax.rem(low + j, LOW)
-        return rcopy(fin.at[low], fin.at[low], b3s.at[j], b3r.at[low], to)
-
-    def fin_in(j):
-        frm = lax.rem(low + j, LOW)
-        return rcopy(fin.at[frm], fin.at[frm], b3s.at[j], b3r.at[frm], left)
-
-    for j in range(1, LOW):
-        big1_copy(j).start()
-    lax.fori_loop(0, rows, put_out, 0)
-    big1[low] = parts[low]
-    for j in range(1, LOW):
-        big1_in(j).wait_recv()
-    tile = big1[0]
-    for l in range(1, LOW):
-        tile = tile + big1[l]
-    big2[high] = tile
-    for j in range(1, n_high):
-        big2_copy(j).start()
-    for j in range(1, n_high):
-        big2_in(j).wait_recv()
-    tile = big2[0]
-    for l in range(1, n_high):
-        tile = tile + big2[l]
-    fin[low] = tile
-    for j in range(1, LOW):
-        fin_copy(j).start()
-    for j in range(1, LOW):
-        fin_in(j).wait_recv()
-
+        parts[2 * p] = quarters[p][0:kvec // 2]
+        parts[2 * p + 1] = quarters[p][kvec // 2:]
+    later.start()
+    later.middle()
+    top, bottom = red_end(ITERS)
+    sums_out[...] = jnp.broadcast_to(top / (bottom + 1.0), (kvec, 128))
+    later.back()
     for p in range(8):
-        mats[p] = fin[p]
+        early_out[p] = early3[p]
+    later.end()
+    for p in range(8):
+        late_out[p] = fin[p]
     pltpu.make_async_copy(fc, fc, out_sem.at[0]).wait()
     pltpu.make_async_copy(fu, fu, out_sem.at[1]).wait()
 
-    for j in range(1, LOW):
-        big1_copy(j).wait_send()
-        fin_copy(j).wait_send()
-    for j in range(1, n_high):
-        big2_copy(j).wait_send()
+    soon.drain()
+    later.drain()
     z_copy(0).wait_send()
     for n in range(ITERS + 1):
         spill_copy(n).wait_send()
 
 
-def finish(kvec, c_in, u_in, fin, corr, reduced, cbuf, ubuf, aug, sem):
+def finish(kvec, c_in, u_in, early, late, step_in, corr, reduced, cbuf, ubuf, aug, sem):
     first = pltpu.make_async_copy(c_in, cbuf, sem.at[0])
     second = pltpu.make_async_copy(u_in, ubuf, sem.at[1])
+    third = pltpu.make_async_copy(cbuf, corr, sem.at[2])
     first.start()
     second.start()
-    head = fin[0]
-    step = head[:, 96:97] / (head[:, 97:98] + 1.0)
-    wide = jnp.broadcast_to(step, (kvec, 512))
-    first.wait()
-    second.wait()
-
-    def add(g, c):
-        at = pl.ds(pl.multiple_of(g * 512, 512), 512)
-        cbuf[:, at] = cbuf[:, at] + wide * ubuf[:, at]
-        return c
-
-    lax.fori_loop(0, cbuf.shape[1] // 512, add, 0)
-    third = pltpu.make_async_copy(cbuf, corr, sem.at[2])
-    third.start()
-    full = reduce_basis([fin[p] for p in range(4)], [fin[p] for p in range(4, 8)], step, aug, kvec)
+    step = step_in[:, 0:1]
+
+    def add_last():
+        wide = jnp.broadcast_to(step, (kvec, 512))
+        first.wait()
+        second.wait()
+
+        def add(g, c):
+            at = pl.ds(pl.multiple_of(g * 512, 512), 512)
+            cbuf[:, at] = cbuf[:, at] + wide * ubuf[:, at]
+            return c
+
+        lax.fori_loop(0, cbuf.shape[1] // 512, add, 0)
+        third.start()
+
+    quarter = lambda p: jnp.concatenate([late[2 * p], late[2 * p + 1]], axis=0)
+    half = lambda g: jnp.concatenate([early[4 * g + p] for p in range(4)], axis=0)
+    full = reduce_basis([half(0), half(1)], [quarter(p) for p in range(4)], step, aug, kvec, add_last)
     reduced[...] = full[:, 0:3 * kvec]
     third.wait()
 
@@ -562,15 +630,17 @@
     def run(*args):
         return kernel(n_dev, rows, kvec, bs, *args)
 
-    mid, last, mats = pl.pallas_call(
+    outs = pl.pallas_call(
         run,
         out_shape=(
             jax.ShapeDtypeStruct(vectors.shape, F32),
             jax.ShapeDtypeStruct(vectors.shape, F32),
-            jax.ShapeDtypeStruct((8, kvec, 128), F32),
+            jax.ShapeDtypeStruct((8, 8, 128), F32),
+            jax.ShapeDtypeStruct((8, kvec // 2, 128), F32),
+            jax.ShapeDtypeStruct((kvec, 128), F32),
         ),
         in_specs=[smem, smem, hbm, vmem, hbm, hbm, hbm, hbm],
-        out_specs=(hbm, hbm, vmem),
+        out_specs=(hbm, hbm, vmem, vmem, vmem),
         scratch_shapes=[
             pltpu.VMEM((STAGES, slots, bs, bs), F32),
             tiles, tiles, tiles, tiles,
@@ -591,16 +661,21 @@
             pltpu.VMEM((HB, 2 * kvec, bs), F32),
             pltpu.VMEM((HB, 2 * kvec, bs), F32),
             pltpu.VMEM((HB, 2 * kvec, bs), F32),
-            pltpu.VMEM((ITERS, LOW, 8, 128), F32),
-            pltpu.VMEM((ITERS, n_high, 8, 128), F32),
+            pltpu.VMEM((ITERS + 1, LOW, 8, 128), F32),
+            pltpu.VMEM((ITERS + 1, n_high, 8, 128), F32),
             pltpu.VMEM((4 * kvec, 256), F32),
-            pltpu.VMEM((8, kvec, 128), F32),
-            pltpu.VMEM((LOW, kvec, 128), F32),
-            pltpu.VMEM((n_high, kvec, 128), F32),
-            pltpu.VMEM((8, kvec, 128), F32),
+            pltpu.VMEM((LOW, 8, 128), F32),
+            pltpu.VMEM((LOW, 8, 128), F32),
+            pltpu.VMEM((n_high, 8, 128), F32),
+            pltpu.VMEM((LOW, 8, 128), F32),
+            pltpu.VMEM((LOW, kvec // 2, 128), F32),
+            pltpu.VMEM((LOW, kvec // 2, 128), F32),
+            pltpu.VMEM((n_high, kvec // 2, 128), F32),
+            pltpu.VMEM((LOW, kvec // 2, 128), F32),
             dma((STAGES,)), dma((3,)), dma((2,)),
             dma((ITERS + 1,)), dma((ITERS + 1,)), dma((ITERS + 1,)), dma((ITERS + 1,)),
-            dma((ITERS, LOW)), dma((ITERS, LOW)), dma((ITERS, n_high)), dma((ITERS, n_high)),
+            dma((ITERS + 1, LOW)), dma((ITERS + 1, LOW)), dma((ITERS + 1, n_high)), dma((ITERS + 1, n_high)),
+            dma((LOW,)), dma((LOW,)), dma((n_high,)), dma((n_high,)), dma((LOW,)), dma((LOW,)),
             dma((LOW,)), dma((LOW,)), dma((n_high,)), dma((n_high,)), dma((LOW,)), dma((LOW,)),
         ],
         compiler_params=pltpu.CompilerParams(
@@ -617,7 +692,7 @@
             jax.ShapeDtypeStruct(vectors.shape, F32),
             jax.ShapeDtypeStruct((3 * kvec, 3 * kvec), F32),
         ),
-        in_specs=[hbm, hbm, vmem],
+        in_specs=[hbm, hbm, vmem, vmem, vmem],
         out_specs=(hbm, vmem),
         scratch_shapes=[
             pltpu.VMEM(vectors.shape, F32),
@@ -625,7 +700,7 @@
             pltpu.VMEM((3 * kvec, 256), F32),
             dma((3,)),
         ],
-    )(mid, last, mats)
+    )(*outs)
 
 
 def solution(mesh):

time: 77.3 us -> 79.8 us (1.032)
  Pallas kernels: 75.3 us -> 77.7 us
    pallas_call x1, Pallas kernels: 69.2 us -> 72.2 us  [local(): pl.pallas_call(run, out_shape=(jax.ShapeDtypeStruct(vectors.shape, F32),...]
where the time goes in v4:
time: 79.8 us; the launch traced here: 78.5 us
  Pallas kernels  77.7 us (97%)
  between operations  0.82 us (1%)
    pallas_call x1, Pallas kernels, local(): pl.pallas_call(run, out_shape=(jax.ShapeDtypeStruct(vectors.shape, F32),...  72.2 us
    pallas_call x1, Pallas kernels, local(): pl.pallas_call(run_last, out_shape=(jax.ShapeDtypeStruct(vectors.shape, F...  5.55 us

profile of v4, /device:TPU:0, one launch (start us, length us, event | category | flops | bytes accessed | tf_op | source)
XLA Modules:
  0.0 78.5 jit_solution(16211728203671231525)
XLA Ops:
  0.6 72.2 %shard_map.95 = (f32[32,4096]{1,0:T(8,128)}, f32[32,4096]{1,0:T(8,128)}, f32[8,8,128]{2,1,0:T(8,128)}, f32[8,16,128]{2,1,0:T(8,128)}, f32[32,128]{1,0:T(8,128)}) custom-call(s32[4,16]{1,0:T(4,128)} %bitcast.3, s32[16]{0:T(128)} %args_1_.4, f32[16,4,256,256]{3,2,1,0:T(8,128)} %args_2_.4, f32[16,1,256]{2,1,0:T(1,128)} %bitcast.2, f32[16,256,256]{2,1,0:T(8,128)} %args_4_.4, ...), custom_call_target="tpu_custom_call" | custom-call | tf_op jit(solution)/shard_map/pallas_call | solution.py:633
  72.8 5.6 %shard_map.96 = (f32[32,4096]{1,0:T(8,128)}, f32[96,96]{1,0:T(8,128)}) custom-call(f32[32,4096]{1,0:T(8,128)} %get-tuple-element.7.args_0_, f32[32,4096]{1,0:T(8,128)} %get-tuple-element.8.args_1_, f32[8,8,128]{2,1,0:T(8,128)} %get-tuple-element.9.args_2_, f32[8,16,128]{2,1,0:T(8,128)} %get-tuple-element.10.args_3_, f32[32,128]{1,0:T(8,128)} %get-tuple-element.11.args_4_), custom_call_target="tpu_custom_call" | custom-call | tf_op jit(solution)/shard_map/pallas_call | solution.py:689

commit v5 on v4

--- a/solution.py
+++ b/solution.py
@@ -103,9 +103,9 @@
 
 def kernel(
     n_dev, rows, kvec, bs,
-    cols, live, blocks, onsite, precond, vec, pvec, pimg,
+    cols_in, live_in, blocks, onsite_in, precond, vec, pvec, pimg,
     c_out, u_out, early_out, late_out, sums_out,
-    stage, bh, bl, th, tl, ph, plo, offs,
+    cols, live, onsite, stage, bh, bl, th, tl, ph, plo, offs,
     fw, fhw, fpv, fpi, fim, fr, fu, fhu, fa, fz, fc, fh, zsw, accw, zs, acc, qb, sb,
     zhalo, inc, spill, zhalo0, inc0, spill0, red1, red2, gram, early, early1, early2, early3, parts, big1, big2, fin,
     stage_sem, load_sem, out_sem, zs_sem, zr_sem, ss_sem, sr_sem,
@@ -135,9 +135,29 @@
         pltpu.make_async_copy(vec.at[:, at], fw.at[b, pl.ds(0, kvec)], load_sem.at[0]).start()
         return c
 
+    smalls = [
+        pltpu.make_async_copy(x, y, load_sem.at[3 + t])
+        for t, (x, y) in enumerate(((cols_in, cols), (live_in, live), (onsite_in, onsite)))
+    ]
     lax.fori_loop(0, rows, start_loads, 0)
     for j in range(STAGES):
         precond_copy(j).start()
+    for copy in smalls:
+        copy.start()
+
+    barrier = pltpu.get_barrier_semaphore()
+    others = n_dev // 2
+
+    def greet(j, c):
+        pl.semaphore_signal(barrier, inc=1, device_id=(lax.rem(me + 2 * j, n_dev),), device_id_type=MESH)
+        return c
+
+    lax.fori_loop(1, others, greet, 0)
+    partner = me + 1 - 2 * lax.rem(me, 2)
+    near_odd = [high * LOW + lax.rem(low + j, LOW) for j in range(1, LOW, 2)]
+    for peer in [left, right] + near_odd:
+        pl.semaphore_signal(barrier, inc=1, device_id=(peer,), device_id_type=MESH)
+    n_greet = others - 1 + 2 + len(near_odd)
 
     def start_more(b, c):
         at = pl.ds(pl.multiple_of(b * bs, bs), bs)
@@ -145,13 +165,6 @@
         pltpu.make_async_copy(pimg.at[:, at], fpi.at[b], load_sem.at[2]).start()
         return c
 
-    barrier = pltpu.get_barrier_semaphore()
-    peers = [left, right]
-    peers += [high * LOW + lax.rem(low + j, LOW) for j in range(1, LOW)]
-    peers += [lax.rem(high + j, n_high) * LOW + low for j in range(1, n_high)]
-    for peer in peers:
-        pl.semaphore_signal(barrier, inc=1, device_id=(peer,), device_id_type=MESH)
-
     def rcopy(src, dst, s_sem, r_sem, to):
         return pltpu.make_async_remote_copy(
             src_ref=src, dst_ref=dst, send_sem=s_sem, recv_sem=r_sem,
@@ -166,67 +179,40 @@
         src, dst = (spill0, inc0) if n == 0 else (spill.at[n - 1], inc.at[n - 1])
         return rcopy(src, dst, ss_sem.at[n], sr_sem.at[n], right)
 
-    def low_copy(i, j):
-        to = high * LOW + lax.rem(low + j, LOW)
-        return rcopy(red1.at[i, low], red1.at[i, low], r1s.at[i, j], r1r.at[i, low], to)
-
-    def low_in(i, j):
-        frm = lax.rem(low + j, LOW)
-        return rcopy(red1.at[i, frm], red1.at[i, frm], r1s.at[i, j], r1r.at[i, frm], left)
-
-    def high_copy(i, j):
-        to = lax.rem(high + j, n_high) * LOW + low
-        return rcopy(red2.at[i, high], red2.at[i, high], r2s.at[i, j], r2r.at[i, high], to)
-
-    def high_in(i, j):
-        frm = lax.rem(high + j, n_high)
-        return rcopy(red2.at[i, frm], red2.at[i, frm], r2s.at[i, j], r2r.at[i, frm], left)
-
-    lane = lax.broadcasted_iota(jnp.int32, (8, 128), 1)
-    groups = kvec // 8
-
-    def pack(a, b):
-        tile = jnp.zeros((8, 128), F32)
-        for g in range(groups):
-            tile = tile + jnp.where(lane == g, a[8 * g:8 * g + 8], 0.0)
-            tile = tile + jnp.where(lane == groups + g, b[8 * g:8 * g + 8], 0.0)
-        return tile
-
-    def unpack(tile):
-        out = []
-        for base in (0, groups):
-            out.append(jnp.concatenate(
-                [jnp.sum(jnp.where(lane == base + g, tile, 0.0), axis=1, keepdims=True) for g in range(groups)],
-                axis=0,
-            ))
-        return out
+    def pair_copy(i):
+        return rcopy(red1.at[i, 0], red1.at[i, 1], r1s.at[i], r1r.at[i], partner)
+
+    def chip_copy(i, j):
+        at = red2.at[i, lax.div(me, 2)]
+        return rcopy(at, at, r2s.at[i], r2r.at[i], lax.rem(me + 2 * j, n_dev))
+
+    span = lax.broadcasted_iota(jnp.int32, (kvec, 128), 1)
+    rank = lax.broadcasted_iota(jnp.int32, (kvec, 128), 0)
 
     def red_start(i, a, b):
-        red1[i, low] = pack(a, b)
-        for j in range(1, LOW):
-            low_copy(i, j).start()
+        both = jnp.where(span == rank, a, 0.0) + jnp.where(span == rank + kvec, b, 0.0)
+        red1[i, 0] = jnp.sum(both, axis=0, keepdims=True)
+        pair_copy(i).start()
 
     def red_mid(i):
-        for j in range(1, LOW):
-            low_in(i, j).wait_recv()
-        tile = red1[i, 0]
-        for l in range(1, LOW):
-            tile = tile + red1[i, l]
-        red2[i, high] = tile
-        for j in range(1, n_high):
-            high_copy(i, j).start()
+        pair_copy(i).wait_recv()
+        red2[i, lax.div(me, 2)] = red1[i, 0] + red1[i, 1]
+
+        def send(j, c):
+            chip_copy(i, j).start()
+            return c
+
+        lax.fori_loop(1, others, send, 0)
 
     def red_end(i):
-        for j in range(1, n_high):
-            high_in(i, j).wait_recv()
-        tile = red2[i, 0]
-        for l in range(1, n_high):
-            tile = tile + red2[i, l]
-        for j in range(1, LOW):
-            low_copy(i, j).wait_send()
-        for j in range(1, n_high):
-            high_copy(i, j).wait_send()
-        return unpack(tile)
+        got = red2.at[i, pl.ds(0, others - 1)]
+        pltpu.make_async_copy(got, got, r2r.at[i]).wait()
+        pltpu.make_async_copy(got, got, r2s.at[i]).wait()
+        pair_copy(i).wait_send()
+        line = jnp.broadcast_to(jnp.sum(red2[i], axis=0), (kvec, 128))
+        top = jnp.sum(jnp.where(span == rank, line, 0.0), axis=1, keepdims=True)
+        bottom = jnp.sum(jnp.where(span == rank + kvec, line, 0.0), axis=1, keepdims=True)
+        return top, bottom
 
     class Exchange:
         def __init__(self, src, near, far, out, sems):
@@ -361,6 +347,8 @@
         return part[0:kvec] + part[kvec:] + mm(dh, plo[b])
 
     pltpu.make_async_copy(fw.at[:, pl.ds(0, kvec)], fw.at[:, pl.ds(0, kvec)], load_sem.at[0]).wait()
+    for copy in smalls:
+        copy.wait()
     for j in range(rows // SLOTS):
         precond_copy(j).wait()
         for t in range(SLOTS):
@@ -376,9 +364,6 @@
             x = fw[b]
             wide.put(b, x)
             wide.diag(b, x)
-        if j == 0:
-            pl.semaphore_wait(barrier, len(peers))
-            z_copy(0).start()
     lax.fori_loop(0, rows, start_more, 0)
     wide.clear_tail()
 
@@ -402,6 +387,8 @@
         return c
 
     lax.fori_loop(0, HB, tail_row, 0)
+    pl.semaphore_wait(barrier, n_greet)
+    z_copy(0).start()
     wide.send_spill(0)
 
     def head_row(b, c):
@@ -465,6 +452,7 @@
         thin.clear_tail()
         for b in range(edge, rows):
             prepare(b)
+        red_mid(k)
         for b in range(edge, rows):
             thin.onto(b)
         thin.send_spill(n)
@@ -476,7 +464,6 @@
 
         for g in range((edge - HB) // 4):
             interior(g, 0)
-        red_mid(k)
         (soon.middle, soon.back, soon.end)[k]()
 
         def body(g, c):
@@ -554,8 +541,6 @@
         return c
 
     lax.fori_loop(0, rows, products, 0)
-    red_mid(ITERS)
-    span = lax.broadcasted_iota(jnp.int32, (kvec, 128), 1)
     hp = pltpu.roll(gram[2 * kvec:3 * kvec, 0:128], 64, 1)
     hup = pltpu.roll(gram[3 * kvec:4 * kvec, 0:128], 64, 1)
     last = span >= 3 * kvec
@@ -569,6 +554,7 @@
         parts[2 * p] = quarters[p][0:kvec // 2]
         parts[2 * p + 1] = quarters[p][kvec // 2:]
     later.start()
+    red_mid(ITERS)
     later.middle()
     top, bottom = red_end(ITERS)
     sums_out[...] = jnp.broadcast_to(top / (bottom + 1.0), (kvec, 128))
@@ -624,7 +610,6 @@
     tiles = pltpu.VMEM((rows * slots, bs, bs), BF16)
     dma = pltpu.SemaphoreType.DMA
     hbm = pl.BlockSpec(memory_space=pl.ANY)
-    smem = pl.BlockSpec(memory_space=pltpu.SMEM)
     vmem = pl.BlockSpec(memory_space=pltpu.VMEM)
 
     def run(*args):
@@ -639,9 +624,12 @@
             jax.ShapeDtypeStruct((8, kvec // 2, 128), F32),
             jax.ShapeDtypeStruct((kvec, 128), F32),
         ),
-        in_specs=[smem, smem, hbm, vmem, hbm, hbm, hbm, hbm],
+        in_specs=[hbm] * 8,
         out_specs=(hbm, hbm, vmem, vmem, vmem),
         scratch_shapes=[
+            pltpu.SMEM((slots, rows), jnp.int32),
+            pltpu.SMEM((rows,), jnp.int32),
+            pltpu.VMEM((rows, 1, bs), F32),
             pltpu.VMEM((STAGES, slots, bs, bs), F32),
             tiles, tiles, tiles, tiles,
             pltpu.VMEM((rows, bs, bs), BF16),
@@ -661,8 +649,8 @@
             pltpu.VMEM((HB, 2 * kvec, bs), F32),
             pltpu.VMEM((HB, 2 * kvec, bs), F32),
             pltpu.VMEM((HB, 2 * kvec, bs), F32),
-            pltpu.VMEM((ITERS + 1, LOW, 8, 128), F32),
-            pltpu.VMEM((ITERS + 1, n_high, 8, 128), F32),
+            pltpu.VMEM((ITERS + 1, 2, 1, 128), F32),
+            pltpu.VMEM((ITERS + 1, n_dev // 2, 1, 128), F32),
             pltpu.VMEM((4 * kvec, 256), F32),
             pltpu.VMEM((LOW, 8, 128), F32),
             pltpu.VMEM((LOW, 8, 128), F32),
@@ -672,9 +660,9 @@
             pltpu.VMEM((LOW, kvec // 2, 128), F32),
             pltpu.VMEM((n_high, kvec // 2, 128), F32),
             pltpu.VMEM((LOW, kvec // 2, 128), F32),
-            dma((STAGES,)), dma((3,)), dma((2,)),
+            dma((STAGES,)), dma((6,)), dma((2,)),
             dma((ITERS + 1,)), dma((ITERS + 1,)), dma((ITERS + 1,)), dma((ITERS + 1,)),
-            dma((ITERS + 1, LOW)), dma((ITERS + 1, LOW)), dma((ITERS + 1, n_high)), dma((ITERS + 1, n_high)),
+            dma((ITERS + 1,)), dma((ITERS + 1,)), dma((ITERS + 1,)), dma((ITERS + 1,)),
             dma((LOW,)), dma((LOW,)), dma((n_high,)), dma((n_high,)), dma((LOW,)), dma((LOW,)),
             dma((LOW,)), dma((LOW,)), dma((n_high,)), dma((n_high,)), dma((LOW,)), dma((LOW,)),
         ],

time: 79.8 us -> 75.5 us (0.946)
  Pallas kernels: 77.7 us -> 73.5 us
    pallas_call x1, Pallas kernels: 72.2 us -> 67.9 us  [local(): pl.pallas_call(run, out_shape=(jax.ShapeDtypeStruct(vectors.shape, F32),...]
where the time goes in v5:
time: 75.5 us; the launch traced here: 74.3 us
  Pallas kernels  73.5 us (97%)
  between operations  0.8 us (1%)
    pallas_call x1, Pallas kernels, local(): pl.pallas_call(run, out_shape=(jax.ShapeDtypeStruct(vectors.shape, F32),...  67.9 us
    pallas_call x1, Pallas kernels, local(): pl.pallas_call(run_last, out_shape=(jax.ShapeDtypeStruct(vectors.shape, F...  5.55 us

profile of v5, /device:TPU:0, one launch (start us, length us, event | category | flops | bytes accessed | tf_op | source)
XLA Modules:
  0.0 74.3 jit_solution(3924560922238698231)
XLA Ops:
  0.6 67.9 %shard_map.95 = (f32[32,4096]{1,0:T(8,128)}, f32[32,4096]{1,0:T(8,128)}, f32[8,8,128]{2,1,0:T(8,128)}, f32[8,16,128]{2,1,0:T(8,128)}, f32[32,128]{1,0:T(8,128)}) custom-call(s32[4,16]{1,0:T(4,128)} %bitcast.3, s32[16]{0:T(128)} %args_1_.4, f32[16,4,256,256]{3,2,1,0:T(8,128)} %args_2_.4, f32[16,1,256]{2,1,0:T(1,128)} %bitcast.2, f32[16,256,256]{2,1,0:T(8,128)} %args_4_.4, ...), custom_call_target="tpu_custom_call" | custom-call | tf_op jit(solution)/shard_map/pallas_call | solution.py:618
  68.6 5.6 %shard_map.96 = (f32[32,4096]{1,0:T(8,128)}, f32[96,96]{1,0:T(8,128)}) custom-call(f32[32,4096]{1,0:T(8,128)} %get-tuple-element.7.args_0_, f32[32,4096]{1,0:T(8,128)} %get-tuple-element.8.args_1_, f32[8,8,128]{2,1,0:T(8,128)} %get-tuple-element.9.args_2_, f32[8,16,128]{2,1,0:T(8,128)} %get-tuple-element.10.args_3_, f32[32,128]{1,0:T(8,128)} %get-tuple-element.11.args_4_), custom_call_target="tpu_custom_call" | custom-call | tf_op jit(solution)/shard_map/pallas_call | solution.py:677

commit v6 on v5

--- a/solution.py
+++ b/solution.py
@@ -198,11 +198,8 @@
         pair_copy(i).wait_recv()
         red2[i, lax.div(me, 2)] = red1[i, 0] + red1[i, 1]
 
-        def send(j, c):
+        for j in range(1, others):
             chip_copy(i, j).start()
-            return c
-
-        lax.fori_loop(1, others, send, 0)
 
     def red_end(i):
         got = red2.at[i, pl.ds(0, others - 1)]
@@ -377,8 +374,8 @@
             xh, xl = split(stage[slot, s] * alive)
             bh[b * SLOTS + s] = xh
             bl[b * SLOTS + s] = xl
-            th[b * SLOTS + s] = xh.T
-            tl[b * SLOTS + s] = xl.T
+            th[b * SLOTS + s] = bh[b * SLOTS + s].T
+            tl[b * SLOTS + s] = bl[b * SLOTS + s].T
 
     def tail_row(i, c):
         take_row(edge + i, i)
@@ -464,7 +461,6 @@
 
         for g in range((edge - HB) // 4):
             interior(g, 0)
-        (soon.middle, soon.back, soon.end)[k]()
 
         def body(g, c):
             for t in range(4):
@@ -480,6 +476,7 @@
             thin.across(b)
         thin.take_in(n)
         z_copy(n).wait_send()
+        (soon.middle, soon.back, soon.end)[k]()
         top, bottom = red_end(k)
         if k == 0:
             qb[...] = jnp.broadcast_to(top / bottom, (kvec, bs))
@@ -528,19 +525,23 @@
     red_start(ITERS, total_of(cross), total_of(own))
     lax.fori_loop(0, rows, put_out, 0)
 
-    gram[...] = jnp.zeros_like(gram)
-
-    def products(b, c):
+    def product_of(b):
         xh, xl = split(jnp.concatenate([fw[b, 0:kvec], fpv[b], fc[b], fu[b]], axis=0))
         yh, yl = split(jnp.concatenate([fim[b], fpi[b], fh[b], fhu[b]], axis=0))
         m = 2 * kvec
+        n = 2 * m
         left_side = jnp.concatenate([xh[m:], yh[m:], xl[m:], yl[m:]], axis=0)
         part = mmt(left_side, jnp.concatenate([xh, yh], axis=0))
-        n = 2 * m
-        gram[...] = gram[...] + (part[0:n] + part[n:] + mmt(left_side[0:n], jnp.concatenate([xl, yl], axis=0)))
+        return part[0:n], part[n:], mmt(left_side[0:n], jnp.concatenate([xl, yl], axis=0))
+
+    gram[...] = jnp.zeros_like(gram)
+
+    def products(g, c):
+        one, two = product_of(2 * g), product_of(2 * g + 1)
+        gram[...] = gram[...] + ((one[0] + two[0]) + (one[1] + two[1]) + (one[2] + two[2]))
         return c
 
-    lax.fori_loop(0, rows, products, 0)
+    lax.fori_loop(0, rows // 2, products, 0)
     hp = pltpu.roll(gram[2 * kvec:3 * kvec, 0:128], 64, 1)
     hup = pltpu.roll(gram[3 * kvec:4 * kvec, 0:128], 64, 1)
     last = span >= 3 * kvec

time: 75.5 us -> 72.2 us (0.956)
  Pallas kernels: 73.5 us -> 70.2 us
    pallas_call x1, Pallas kernels: 67.9 us -> 64.7 us  [local(): pl.pallas_call(run, out_shape=(jax.ShapeDtypeStruct(vectors.shape, F32),...]
where the time goes in v6:
time: 72.2 us; the launch traced here: 71 us
  Pallas kernels  70.2 us (97%)
  between operations  0.82 us (1%)
    pallas_call x1, Pallas kernels, local(): pl.pallas_call(run, out_shape=(jax.ShapeDtypeStruct(vectors.shape, F32),...  64.7 us
    pallas_call x1, Pallas kernels, local(): pl.pallas_call(run_last, out_shape=(jax.ShapeDtypeStruct(vectors.shape, F...  5.55 us

profile of v6, /device:TPU:0, one launch (start us, length us, event | category | flops | bytes accessed | tf_op | source)
XLA Modules:
  0.0 71.0 jit_solution(11518844127379520054)
XLA Ops:
  0.6 64.7 %shard_map.95 = (f32[32,4096]{1,0:T(8,128)}, f32[32,4096]{1,0:T(8,128)}, f32[8,8,128]{2,1,0:T(8,128)}, f32[8,16,128]{2,1,0:T(8,128)}, f32[32,128]{1,0:T(8,128)}) custom-call(s32[4,16]{1,0:T(4,128)} %bitcast.3, s32[16]{0:T(128)} %args_1_.4, f32[16,4,256,256]{3,2,1,0:T(8,128)} %args_2_.4, f32[16,1,256]{2,1,0:T(1,128)} %bitcast.2, f32[16,256,256]{2,1,0:T(8,128)} %args_4_.4, ...), custom_call_target="tpu_custom_call" | custom-call | tf_op jit(solution)/shard_map/pallas_call | solution.py:619
  65.3 5.6 %shard_map.96 = (f32[32,4096]{1,0:T(8,128)}, f32[96,96]{1,0:T(8,128)}) custom-call(f32[32,4096]{1,0:T(8,128)} %get-tuple-element.7.args_0_, f32[32,4096]{1,0:T(8,128)} %get-tuple-element.8.args_1_, f32[8,8,128]{2,1,0:T(8,128)} %get-tuple-element.9.args_2_, f32[8,16,128]{2,1,0:T(8,128)} %get-tuple-element.10.args_3_, f32[32,128]{1,0:T(8,128)} %get-tuple-element.11.args_4_), custom_call_target="tpu_custom_call" | custom-call | tf_op jit(solution)/shard_map/pallas_call | solution.py:678

commit v7 on v6

--- a/solution.py
+++ b/solution.py
@@ -300,15 +300,12 @@
 
         def onto(self, b):
             zb = self.zs[b]
-            sums = [None] * (HB + 1)
-            for s in range(SLOTS):
-                moved = self.product(zb, bh[b * SLOTS + s], bl[b * SLOTS + s])
-                off = offs[b * SLOTS + s]
-                for o in range(HB + 1):
-                    term = jnp.where(off == o, 1.0, 0.0) * moved
-                    sums[o] = term if sums[o] is None else sums[o] + term
+            moved = [self.product(zb, bh[b * SLOTS + s], bl[b * SLOTS + s]) for s in range(SLOTS)]
             for o in range(HB + 1):
-                self.acc[b + o] = self.acc[b + o] + sums[o]
+                total_o = self.acc[b + o]
+                for s in range(SLOTS):
+                    total_o = total_o + jnp.where(offs[b * SLOTS + s] == o, 1.0, 0.0) * moved[s]
+                self.acc[b + o] = total_o
 
         def across(self, b):
             out = None

time: 72.2 us -> 72.3 us (level)
  no operation moved by 1% of the time
where the time goes in v7:
time: 72.3 us; the launch traced here: 71.1 us
  Pallas kernels  70.3 us (97%)
  between operations  0.82 us (1%)
    pallas_call x1, Pallas kernels, local(): pl.pallas_call(run, out_shape=(jax.ShapeDtypeStruct(vectors.shape, F32),...  64.8 us
    pallas_call x1, Pallas kernels, local(): pl.pallas_call(run_last, out_shape=(jax.ShapeDtypeStruct(vectors.shape, F...  5.56 us

profile of v7, /device:TPU:0, one launch (start us, length us, event | category | flops | bytes accessed | tf_op | source)
XLA Modules:
  0.0 71.1 jit_solution(16606889445648994881)
XLA Ops:
  0.6 64.8 %shard_map.95 = (f32[32,4096]{1,0:T(8,128)}, f32[32,4096]{1,0:T(8,128)}, f32[8,8,128]{2,1,0:T(8,128)}, f32[8,16,128]{2,1,0:T(8,128)}, f32[32,128]{1,0:T(8,128)}) custom-call(s32[4,16]{1,0:T(4,128)} %bitcast.3, s32[16]{0:T(128)} %args_1_.4, f32[16,4,256,256]{3,2,1,0:T(8,128)} %args_2_.4, f32[16,1,256]{2,1,0:T(1,128)} %bitcast.2, f32[16,256,256]{2,1,0:T(8,128)} %args_4_.4, ...), custom_call_target="tpu_custom_call" | custom-call | tf_op jit(solution)/shard_map/pallas_call | solution.py:616
  65.4 5.6 %shard_map.96 = (f32[32,4096]{1,0:T(8,128)}, f32[96,96]{1,0:T(8,128)}) custom-call(f32[32,4096]{1,0:T(8,128)} %get-tuple-element.7.args_0_, f32[32,4096]{1,0:T(8,128)} %get-tuple-element.8.args_1_, f32[8,8,128]{2,1,0:T(8,128)} %get-tuple-element.9.args_2_, f32[8,16,128]{2,1,0:T(8,128)} %get-tuple-element.10.args_3_, f32[32,128]{1,0:T(8,128)} %get-tuple-element.11.args_4_), custom_call_target="tpu_custom_call" | custom-call | tf_op jit(solution)/shard_map/pallas_call | solution.py:675
